TPU v7x, 32 devices: a whole 2x2x4 slice. The times are simulated.
32 devices in a mesh: rows: 4 (over y, core), cols: 8 (over z, x).
Axes of the slice: x: 2, y: 2, z: 4, core: 2. Of those that a mesh axis runs over, the one named last changes fastest.
Arguments:
- single: bfloat16 [512, 1024], P('rows'), may hold values from -6 to 6
- pair: bfloat16 [512, 512, 128], P('rows', 'cols'), may hold values from -6 to 6
- residue_mask: int32 [512], replicated, may hold values from 0 to 1, as said below
- w_bias: bfloat16 [128, 32], replicated, may hold values from -40 to 40
- w_project: bfloat16 [4, 1024, 1024], P(None, None, 'cols'), may hold values from -0.1875 to 0.1875
- w_out: bfloat16 [1024, 1024], replicated, may hold values from -0.1875 to 0.1875
- w_factors: bfloat16 [1024, 128], replicated, may hold values from -0.1875 to 0.1875
- w_pairout: bfloat16 [128, 128], replicated, may hold values from -0.5 to 0.5
- w_up: bfloat16 [128, 512], replicated, may hold values from -0.5 to 0.5
- w_down: bfloat16 [512, 128], replicated, may hold values from -0.25 to 0.25
Outputs:
- single_out: bfloat16 [512, 1024], P('rows')
- pair_out: bfloat16 [512, 512, 128], P('rows', 'cols')
Inputs may be any that keep to these rules, and one draw needn't show every extreme that they name: residue_mask is 1 on a leading run of at least 256 positions and 0 after it.
All inputs are finite; a program needn't handle non-finite values.
Results may differ from a plain program's by a relative error of at most 0.01.
The roundings to bfloat16 on the way count: a program that leaves them out, or rounds other values in their place, can miss the bound.
Values may be sent and summed in bfloat16 or wider, within the bound.
A program may use at most 64 MiB of HBM per device.

v0:
```python
import functools
import math

import jax
import jax.numpy as jnp
from jax import lax
from jax.experimental import pallas as pl
from jax.experimental.pallas import tpu as pltpu
from jax.sharding import PartitionSpec as P

epsilon = 1e-05


def enter(axes):
    barrier = pltpu.get_barrier_semaphore()
    total = 0
    for axis, size in axes:
        me = lax.axis_index(axis)
        for step in range(1, size):
            pl.semaphore_signal(
                barrier,
                inc=1,
                device_id={axis: lax.rem(me + step, size)},
                device_id_type=pl.DeviceIdType.MESH,
            )
        total += size - 1
    pl.semaphore_wait(barrier, total)


def spread(axis, size, source, landing, send_sems, recv_sems):
    me = lax.axis_index(axis)
    copies = []
    for step in range(1, size):
        copy = pltpu.make_async_remote_copy(
            src_ref=source,
            dst_ref=landing.at[me],
            send_sem=send_sems.at[step - 1],
            recv_sem=recv_sems.at[step - 1],
            device_id={axis: lax.rem(me + step, size)},
            device_id_type=pl.DeviceIdType.MESH,
        )
        copy.start()
        copies.append(copy)
    return copies


def gather_kernel(axis, size, source, gathered, send_sems, recv_sems, own_sem):
    enter([(axis, size)])
    copies = spread(axis, size, source, gathered, send_sems, recv_sems)
    own = pltpu.make_async_copy(source, gathered.at[lax.axis_index(axis)], own_sem)
    own.start()
    own.wait()
    for copy in copies:
        copy.wait()


def gather(values, axis, size, collective_id):
    return pl.pallas_call(
        functools.partial(gather_kernel, axis, size),
        out_shape=jax.ShapeDtypeStruct((size, *values.shape), values.dtype),
        in_specs=[pl.BlockSpec(memory_space=pltpu.VMEM)],
        out_specs=pl.BlockSpec(memory_space=pltpu.VMEM),
        scratch_shapes=[
            pltpu.SemaphoreType.DMA((size - 1,)),
            pltpu.SemaphoreType.DMA((size - 1,)),
            pltpu.SemaphoreType.DMA,
        ],
        compiler_params=pltpu.CompilerParams(collective_id=collective_id, has_side_effects=True),
        name="gather_" + axis,
    )(values)


def single_kernel(
    row_size, col_size, tile_cols,
    mixed, single, w_out, w_factors, single_out, left_out, right_out,
    gathered, factor_right, send_sems, recv_sems, row_send, row_recv, own_sem,
):
    enter([("cols", col_size), ("rows", row_size)])
    tile_rows, width = mixed.shape
    me_col = lax.axis_index("cols")
    me_row = lax.axis_index("rows")
    copies = spread("cols", col_size, mixed, gathered, send_sems, recv_sems)
    own = pltpu.make_async_copy(mixed, gathered.at[me_col], own_sem)
    own.start()
    own.wait()
    for copy in copies:
        copy.wait()
    whole = jnp.concatenate([gathered[part] for part in range(col_size)], axis=1)
    total = jnp.dot(whole, w_out[...], preferred_element_type=jnp.float32)
    updated = (single[...].astype(jnp.float32) + total).astype(jnp.bfloat16)
    single_out[...] = updated
    normed = layer_norm(updated).astype(jnp.bfloat16)
    factors = jnp.dot(normed, w_factors[...], preferred_element_type=jnp.float32)
    factors = factors.astype(jnp.bfloat16).astype(jnp.float32)
    half = factors.shape[1] // 2
    swapped = jnp.concatenate([factors[:, half:], factors[:, :half]], axis=1)
    lower = lax.broadcasted_iota(jnp.int32, factors.shape, 1) < half
    left_out[...] = jnp.where(lower, factors, swapped)
    factor_right[...] = jnp.where(lower, swapped, factors).astype(jnp.bfloat16)
    first = me_col * tile_cols
    owner = first // tile_rows
    offset = pl.multiple_of(first - owner * tile_rows, tile_cols)
    piece = factor_right.at[pl.ds(offset, tile_cols)]

    @pl.when(me_row == owner)
    def _():
        local = pltpu.make_async_copy(piece, right_out, own_sem)
        local.start()
        sends = []
        for step in range(1, row_size):
            send = pltpu.make_async_remote_copy(
                src_ref=piece,
                dst_ref=right_out,
                send_sem=row_send.at[step - 1],
                recv_sem=row_recv,
                device_id={"rows": lax.rem(me_row + step, row_size)},
                device_id_type=pl.DeviceIdType.MESH,
            )
            send.start()
            sends.append(send)
        local.wait()
        for send in sends:
            send.wait_send()

    @pl.when(me_row != owner)
    def _():
        pltpu.make_async_remote_copy(
            src_ref=piece,
            dst_ref=right_out,
            send_sem=row_send.at[0],
            recv_sem=row_recv,
            device_id={"rows": lax.rem(me_row + 1, row_size)},
            device_id_type=pl.DeviceIdType.MESH,
        ).wait_recv()


def update_single(mixed, single, w_out, w_factors, row_size, col_size, tile_cols):
    tile_rows, width = single.shape
    wide = w_factors.shape[1]
    return pl.pallas_call(
        functools.partial(single_kernel, row_size, col_size, tile_cols),
        out_shape=(
            jax.ShapeDtypeStruct((tile_rows, width), jnp.bfloat16),
            jax.ShapeDtypeStruct((tile_rows, wide), jnp.float32),
            jax.ShapeDtypeStruct((tile_cols, wide), jnp.bfloat16),
        ),
        in_specs=[pl.BlockSpec(memory_space=pltpu.VMEM)] * 4,
        out_specs=[pl.BlockSpec(memory_space=pltpu.VMEM)] * 3,
        scratch_shapes=[
            pltpu.VMEM((col_size, *mixed.shape), jnp.bfloat16),
            pltpu.VMEM((tile_rows, wide), jnp.bfloat16),
            pltpu.SemaphoreType.DMA((col_size - 1,)),
            pltpu.SemaphoreType.DMA((col_size - 1,)),
            pltpu.SemaphoreType.DMA((row_size - 1,)),
            pltpu.SemaphoreType.DMA,
            pltpu.SemaphoreType.DMA,
        ],
        compiler_params=pltpu.CompilerParams(collective_id=2, has_side_effects=True),
        name="update_single",
    )(mixed, single, w_out, w_factors)


def matmul_norm(values):
    wide = values.shape[1]
    share = jnp.full((2 * wide, wide), 1.0 / wide, jnp.bfloat16)
    mean = jnp.dot(values, share[:wide], preferred_element_type=jnp.float32)
    centred = values.astype(jnp.float32) - mean
    square = centred * centred
    high = square.astype(jnp.bfloat16)
    low = (square - high.astype(jnp.float32)).astype(jnp.bfloat16)
    spread_out = jnp.dot(
        jnp.concatenate([high, low], 1), share, preferred_element_type=jnp.float32
    )
    return (centred * lax.rsqrt(spread_out + epsilon)).astype(jnp.bfloat16)


def norm_kernel(values, normed):
    normed[...] = matmul_norm(values[...])


def norm_rows(values, block):
    spec = pl.BlockSpec((block, values.shape[1]), lambda step: (step, 0))
    return pl.pallas_call(
        norm_kernel,
        out_shape=jax.ShapeDtypeStruct(values.shape, jnp.bfloat16),
        grid=(values.shape[0] // block,),
        in_specs=[spec],
        out_specs=spec,
        name="norm_pair",
    )(values)


def pair_kernel(pair, left, right, w_pairout, w_up, w_down, updated):
    block_rows, tile_cols, wide = pair.shape
    left_wide = left[...][:, None, :]
    right_wide = right[...].astype(jnp.float32)[None, :, :]
    lower = lax.broadcasted_iota(jnp.int32, pair.shape, 2) < wide // 2
    paired = jnp.where(lower, left_wide * right_wide, left_wide - right_wide)
    paired = paired.astype(jnp.bfloat16).reshape(block_rows * tile_cols, wide)
    flat = pair[...].reshape(block_rows * tile_cols, wide).astype(jnp.float32)
    mid = flat + jnp.dot(paired, w_pairout[...], preferred_element_type=jnp.float32)
    mid = mid.astype(jnp.bfloat16)
    normed = matmul_norm(mid)
    hidden = jnp.dot(normed, w_up[...], preferred_element_type=jnp.float32)
    hidden = jnp.maximum(hidden, 0.0).astype(jnp.bfloat16)
    out = mid.astype(jnp.float32) + jnp.dot(
        hidden, w_down[...], preferred_element_type=jnp.float32
    )
    updated[...] = out.astype(jnp.bfloat16).reshape(pair.shape)


def update_pair(pair, left, right, w_pairout, w_up, w_down):
    tile_rows, tile_cols, wide = pair.shape
    block = math.gcd(tile_rows, max(8, 1024 // tile_cols))
    tile = pl.BlockSpec((block, tile_cols, wide), lambda step: (step, 0, 0))

    def whole(array):
        return pl.BlockSpec(array.shape, lambda step: (0, 0))

    return pl.pallas_call(
        pair_kernel,
        out_shape=jax.ShapeDtypeStruct(pair.shape, jnp.bfloat16),
        grid=(tile_rows // block,),
        in_specs=[
            tile,
            pl.BlockSpec((block, wide), lambda step: (step, 0)),
            whole(right),
            whole(w_pairout),
            whole(w_up),
            whole(w_down),
        ],
        out_specs=tile,
        name="update_pair",
    )(pair, left, right, w_pairout, w_up, w_down)


def layer_norm(values):
    values = values.astype(jnp.float32)
    centred = values - jnp.mean(values, -1, keepdims=True)
    return centred * lax.rsqrt(jnp.mean(centred * centred, -1, keepdims=True) + epsilon)


def per_device(
    row_size, col_size,
    single, pair, residue_mask, w_bias, w_project, w_out, w_factors, w_pairout, w_up, w_down
):
    tile_rows = pair.shape[0]
    tile_cols = pair.shape[1]
    normed_pair = norm_rows(
        pair.reshape(tile_rows * tile_cols, pair.shape[2]), math.gcd(tile_rows * tile_cols, 1024)
    ).reshape(pair.shape)
    bias_local = jnp.einsum(
        "rcp,ph->hrc", normed_pair, w_bias, preferred_element_type=jnp.float32
    ).astype(jnp.bfloat16)
    normed_single = layer_norm(single).astype(jnp.bfloat16)
    projected = jnp.einsum(
        "rs,fsc->frc", normed_single, w_project, preferred_element_type=jnp.float32
    )
    query_rows = projected[0].astype(jnp.bfloat16)
    key_local = projected[1].astype(jnp.bfloat16)
    value_local = projected[2].astype(jnp.bfloat16)
    gate_values = jax.nn.sigmoid(projected[3])
    bias_heads = lax.all_to_all(bias_local, "cols", split_axis=0, concat_axis=2, tiled=True)
    both = gather(jnp.concatenate([key_local, value_local], 1), "rows", row_size, 1)
    both = both.reshape(row_size * tile_rows, both.shape[2])
    key_rows, value_rows = both[:, : key_local.shape[1]], both[:, key_local.shape[1] :]
    heads_here = bias_heads.shape[0]
    head_width = query_rows.shape[1] // heads_here
    residues = key_rows.shape[0]
    query_split = query_rows.reshape(tile_rows, heads_here, head_width)
    key_split = key_rows.reshape(residues, heads_here, head_width)
    value_split = value_rows.reshape(residues, heads_here, head_width)
    score_scale = 1.0 / math.sqrt(head_width)
    scores = jnp.einsum(
        "rhd,lhd->hrl", query_split, key_split, preferred_element_type=jnp.float32
    ) * score_scale + bias_heads.astype(jnp.float32)
    key_valid = (residue_mask > 0)[None, None, :]
    scores = jnp.where(key_valid, scores, -jnp.inf)
    weights = jax.nn.softmax(scores, axis=-1).astype(jnp.bfloat16)
    attended = jnp.einsum("hrl,lhd->rhd", weights, value_split, preferred_element_type=jnp.float32)
    attended = attended.reshape(tile_rows, heads_here * head_width)
    mixed = (attended * gate_values).astype(jnp.bfloat16)
    single_out, left, right = update_single(
        mixed, single, w_out, w_factors, row_size, col_size, tile_cols
    )
    return (single_out, update_pair(pair, left, right, w_pairout, w_up, w_down))


def solution(mesh):
    return jax.shard_map(
        functools.partial(per_device, mesh.shape["rows"], mesh.shape["cols"]),
        mesh=mesh,
        in_specs=(
            P("rows", None),
            P("rows", "cols", None),
            P(),
            P(),
            P(None, None, "cols"),
            P(),
            P(),
            P(),
            P(),
            P(),
        ),
        out_specs=(P("rows", None), P("rows", "cols", None)),
        check_vma=False,
    )
```

profile of v0, /device:TPU:0, one launch (start us, length us, event | category | flops | bytes accessed | tf_op | source)
XLA Modules:
  0.0 62.0 jit_solution(652438604577849002)
XLA Ops:
  0.6 0.0 copy-start
  0.6 7.5 %norm_pair.1 = bf16[8192,128]{1,0:T(8,128)(2,1)} custom-call(bf16[8192,128]{1,0:T(8,128)(2,1)} %bitcast.40), custom_call_target="tpu_custom_call" | custom-call | tf_op jit(solution)/shard_map/norm_pair/pallas_call | solution.py:183
  8.1 0.0 copy-done
  8.1 0.0 copy-start.1
  8.1 0.0 copy-start.2
  8.1 3.1 %fusion.7 = bf16[32,128,64]{1,0,2:T(8,128)(2,1)S(1)} fusion(bf16[128,64,128]{2,1,0:T(8,128)(2,1)} %bitcast.39, bf16[128,32]{0,1:T(8,128)(2,1)S(1)} %copy-done), kind=kOutput, calls=%fused_computation.8 | convolution fusion | flops 67371008 | bytes 2629632 | tf_op jit(solution)/shard_map/rcp,ph->hrc/dot_general | solution.py:252
  11.2 1.0 %copy.44 = bf16[32,128,64]{1,2,0:T(8,128)(2,1)} copy(bf16[32,128,64]{1,0,2:T(8,128)(2,1)S(1)} %fusion.7) | data formatting | bytes 1048576 | tf_op jit(solution)/shard_map/convert_element_type | solution.py:254
  12.2 7.3 %all-to-all-start = ((bf16[32,128,64]{1,2,0:T(8,128)(2,1)}), bf16[32,128,64]{1,2,0:T(8,128)(2,1)S(1)}, u32[]{:S(2)}, u32[]{:S(2)}) async-start(bf16[32,128,64]{1,2,0:T(8,128)(2,1)} %copy.44), calls=%async_computation | async-start | bytes 1048576 | tf_op jit(solution)/shard_map/all_to_all | solution.py:263
  19.5 0.0 copy-done.1
  19.5 0.1 convert_reduce_fusion
  19.6 0.2 fusion.12
  19.9 0.0 copy-done.2
  19.9 0.5 copy.38
  20.4 0.0 copy-start.4
  20.4 0.5 fusion.15
  21.0 0.1 copy.39
  21.1 0.6 %pad_maximum_fusion.source = bf16[128,256]{1,0:T(8,128)(2,1)} fusion(bf16[128,128]{1,0:T(8,128)(2,1)S(1)} %get-tuple-element.11, bf16[128,128]{1,0:T(8,128)(2,1)S(1)} %get-tuple-element.12), kind=kLoop, calls=%fused_computation.27 | loop fusion | flops 131072 | bytes 131072 | tf_op jit(solution)/shard_map/concatenate | solution.py:264
  21.8 6.6 %gather_rows.1 = bf16[4,128,256]{2,1,0:T(8,128)(2,1)} custom-call(bf16[128,256]{1,0:T(8,128)(2,1)} %pad_maximum_fusion.source), custom_call_target="tpu_custom_call" | custom-call | tf_op jit(solution)/shard_map/gather_rows/pallas_call | solution.py:58
  28.3 1.0 %fusion.27 = (bf16[512,128]{1,0:T(8,128)(2,1)S(1)}, bf16[512,128]{1,0:T(8,128)(2,1)S(1)}) fusion(bf16[512,256]{1,0:T(8,128)(2,1)} %bitcast.45), kind=kLoop, calls=%fused_computation.37 | loop fusion | bytes 524288 | tf_op jit(solution)/shard_map/slice | solution.py:266
  29.3 0.1 copy.42
  29.5 0.1 copy.41
  29.6 0.1 copy.40
  29.7 0.0 copy-done.4
  29.7 4.3 %all-to-all-done = bf16[32,128,64]{1,2,0:T(8,128)(2,1)S(1)} async-done(((bf16[32,128,64]{1,2,0:T(8,128)(2,1)}), bf16[32,128,64]{1,2,0:T(8,128)(2,1)S(1)}, u32[]{:S(2)}, u32[]{:S(2)}) %all-to-all-start) | async-done | bytes 524320 | tf_op jit(solution)/shard_map/all_to_all | solution.py:263
  34.0 0.1 convert_bitcast_fusion
  34.1 0.1 copy.45
  34.2 0.3 copy.46
  34.5 0.3 fusion.6
  34.9 0.3 fusion.29
  35.2 1.0 %fusion.14 = f32[4,32,128]{2,1,0:T(8,128)S(1)} fusion(bf16[512,4,32]{0,2,1:T(8,128)(2,1)S(1)} %bitcast.49, f32[4,128]{1,0:T(4,128)S(1)} %fusion.29, f32[4,128,512]{2,1,0:T(8,128)S(1)} %fusion.6), kind=kOutput, calls=%fused_computation.17 | convolution fusion | flops 17564672 | bytes 1247232 | tf_op jit(solution)/shard_map/hrl,lhd->rhd/dot_general | solution.py:280
  36.2 0.1 copy.47
  36.4 0.7 %fusion.24.mixed = bf16[128,128]{1,0:T(8,128)(2,1)} fusion(f32[128,128]{1,0:T(8,128)S(1)} %copy.47, f32[4,128,128]{2,1,0:T(8,128)S(1)} %bitcast.44), kind=kLoop, calls=%fused_computation.28 | loop fusion | flops 81920 | bytes 163840 | tf_op jit(solution)/shard_map/convert_element_type | solution.py:282
  37.0 13.1 %update_single.1 = (bf16[128,1024]{1,0:T(8,128)(2,1)}, f32[128,128]{1,0:T(8,128)}, bf16[64,128]{1,0:T(8,128)(2,1)}) custom-call(bf16[128,128]{1,0:T(8,128)(2,1)} %fusion.24.mixed, bf16[128,1024]{1,0:T(8,128)(2,1)} %single.1, bf16[1024,1024]{1,0:T(8,128)(2,1)} %w_out.1, bf16[1024,128]{1,0:T(8,128)(2,1)} %w_factors.1), custom_call_target="tpu_custom_call" | custom-call | tf_op jit(solution)/shard_map/update_single/pallas_call | solution.py:140
  50.2 0.0 copy-start.3
  50.2 11.2 %update_pair.1 = bf16[128,64,128]{2,1,0:T(8,128)(2,1)} custom-call(bf16[128,64,128]{2,1,0:T(8,128)(2,1)} %pair.1, f32[128,128]{1,0:T(8,128)} %get-tuple-element.6.left, bf16[64,128]{1,0:T(8,128)(2,1)} %get-tuple-element.7.right, bf16[128,128]{1,0:T(8,128)(2,1)} %w_pairout.1, bf16[128,512]{1,0:T(8,128)(2,1)} %w_up.1, bf16[512,128]{1,0:T(8,128)(2,1)} %w_down.1), custom_call_target="tpu_custom_call" | custom-call | tf_op jit(solution)/shard_map/update_pair/pallas_call | solution.py:220
  61.3 0.0 copy-done.3
  61.3 0.7 %copy.53 = bf16[128,1024]{1,0:T(8,128)(2,1)} copy(bf16[128,1024]{1,0:T(8,128)(2,1)S(1)} %copy-done.3) | data formatting | bytes 524288
  (5 shorter events, 0.0 us)
Async XLA Ops:
  0.6 7.5 %copy-start = (bf16[128,32]{0,1:T(8,128)(2,1)S(1)}, bf16[128,32]{0,1:T(8,128)(2,1)}, u32[]{:S(2)}) copy-start(bf16[128,32]{0,1:T(8,128)(2,1)} %param.13) | copy-start | bytes 24580
  8.1 11.4 %copy-start.1 = (bf16[128,1024]{1,0:T(8,128)(2,1)S(1)}, bf16[128,1024]{1,0:T(8,128)(2,1)}, u32[]{:S(2)}) copy-start(bf16[128,1024]{1,0:T(8,128)(2,1)} %single.1) | copy-start | bytes 786436
  8.1 11.7 %copy-start.2 = (bf16[4,1024,128]{2,1,0:T(8,128)(2,1)S(1)}, bf16[4,1024,128]{2,1,0:T(8,128)(2,1)}, u32[]{:S(2)}) copy-start(bf16[4,1024,128]{2,1,0:T(8,128)(2,1)} %param.14) | copy-start | bytes 3145732
  12.2 21.8 %all-to-all-start = ((bf16[32,128,64]{1,2,0:T(8,128)(2,1)}), bf16[32,128,64]{1,2,0:T(8,128)(2,1)S(1)}, u32[]{:S(2)}, u32[]{:S(2)}) async-start(bf16[32,128,64]{1,2,0:T(8,128)(2,1)} %copy.44), calls=%async_computation | async-start | bytes 1048576 | tf_op jit(solution)/shard_map/all_to_all | solution.py:263
  20.4 9.3 %copy-start.4 = (s32[512]{0:T(512)S(1)}, s32[512]{0:T(512)}, u32[]{:S(2)}) copy-start(s32[512]{0:T(512)} %param.12) | copy-start | bytes 6148
  50.2 11.2 %copy-start.3 = (bf16[128,1024]{1,0:T(8,128)(2,1)S(1)}, bf16[128,1024]{1,0:T(8,128)(2,1)}, u32[]{:S(2)}) copy-start(bf16[128,1024]{1,0:T(8,128)(2,1)} %get-tuple-element.15) | copy-start | bytes 786436
where the time goes:
time: 62.5 us; the launch traced here: 62 us
  Pallas kernels  38.3 us (61%)
  starting transfers between devices  7.28 us (12%)
  matrix products  4.99 us (8%)
  waiting for transfers between devices  4.27 us (7%)
  local copies, waits for them, and re-layouts  4.25 us (7%)
  other arithmetic  2.08 us (3%)
  between operations  0.81 us (1%)
    pallas_call x1, Pallas kernels, update_single(): pl.pallas_call(functools.partial(single_kernel, row_size, col_size, tile_...  13.1 us
    pallas_call x1, Pallas kernels, update_pair(): pl.pallas_call(pair_kernel, out_shape=jax.ShapeDtypeStruct(pair.shape, jn...  11.2 us
    pallas_call x1, Pallas kernels, norm_rows(): pl.pallas_call(norm_kernel, out_shape=jax.ShapeDtypeStruct(values.shape,...  7.48 us
    all_to_all x1, starting transfers between devices, per_device(): lax.all_to_all(bias_local, 'cols', split_axis=0, concat_axis=2, tiled=True)  7.28 us
    pallas_call x1, Pallas kernels, gather(): pl.pallas_call(functools.partial(gather_kernel, axis, size), out_shape=ja...  6.56 us
    all_to_all x1, waiting for transfers between devices, per_device(): lax.all_to_all(bias_local, 'cols', split_axis=0, concat_axis=2, tiled=True)  4.27 us
    dot_general x1, matrix products, per_device(): jnp.einsum('rcp,ph->hrc', normed_pair, w_bias, preferred_element_type=jnp...  3.08 us
    unnamed x12, local copies, waits for them, and re-layouts  1.26 us
  transfers between devices with their start and end apart: 1, of which 1 were waited for; matrix products, arithmetic and copies ran while one was open for 6% of the time, Pallas kernels for 11%

commit v1 on v0

--- a/solution.py
+++ b/solution.py
@@ -286,9 +286,482 @@
     return (single_out, update_pair(pair, left, right, w_pairout, w_up, w_down))
 
 
+LANES = 128
+excluded = -1e30
+
+
+def lane_iota(shape):
+    return lax.broadcasted_iota(jnp.int32, shape, len(shape) - 1)
+
+
+def block_constants(wide, copies):
+    size = wide * copies
+    row = lax.broadcasted_iota(jnp.int32, (size, size), 0)
+    col = lax.broadcasted_iota(jnp.int32, (size, size), 1)
+    same = row // wide == col // wide
+    share = jnp.where(same, 1.0 / wide, 0.0)
+    centre = jnp.where(row == col, 1.0, 0.0) - share
+    return centre.astype(jnp.bfloat16), share.astype(jnp.bfloat16)
+
+
+def norm_centred(values, centre, share):
+    centred = jnp.dot(values, centre, preferred_element_type=jnp.float32)
+    square = centred * centred
+    high = square.astype(jnp.bfloat16)
+    low = (square - high.astype(jnp.float32)).astype(jnp.bfloat16)
+    spread_out = jnp.dot(high, share, preferred_element_type=jnp.float32)
+    spread_out = spread_out + jnp.dot(low, share, preferred_element_type=jnp.float32)
+    return (centred * lax.rsqrt(spread_out + epsilon)).astype(jnp.bfloat16)
+
+
+def attend_kernel(
+    row_size, col_size, heads, tile_cols, stride,
+    single, pair, mask, w_bias, w_project, w_out, w_factors,
+    single_out, left_out, right_out,
+    single_v, pair_v, mask_v, bias_w, project_v, out_v, factors_v, own_single,
+    kv_send, kv_recv, q_recv, gate_send, gate_recv, bias_v, o_send, o_recv,
+    st_send, st_recv, left_send, right_send, left_recv, right_recv, so_send, consts, spread_v,
+    load_sems, pair_sems, col_send, col_recv, fan_send, fan_recv,
+):
+    me_row = lax.axis_index("rows")
+    me_col = lax.axis_index("cols")
+    total = row_size * col_size
+    barrier = pltpu.get_barrier_semaphore()
+    me = me_row * col_size + me_col
+    for step in range(1, total):
+        to = lax.rem(me + step, total)
+        pl.semaphore_signal(
+            barrier,
+            inc=1,
+            device_id={"rows": to // col_size, "cols": lax.rem(to, col_size)},
+            device_id_type=pl.DeviceIdType.MESH,
+        )
+    halves, depth, _, wide = pair.shape
+    tile_rows, width = single.shape
+    group = w_project.shape[2]
+    rows_each = depth // col_size
+    heads_here = heads // col_size
+    head_width = group // heads_here
+    chunk = depth // pair_sems.shape[0]
+    loads = [
+        pltpu.make_async_copy(source, target, load_sems.at[index])
+        for index, (source, target) in enumerate(
+            [(single, single_v)]
+            + [(w_project.at[part], project_v.at[part]) for part in (1, 2, 0, 3)]
+            + [(w_bias, bias_w), (mask, mask_v)]
+            + [
+                (single.at[pl.ds(half * depth + me_col * rows_each, rows_each)], own_single.at[half])
+                for half in range(halves)
+            ]
+            + [(w_out, out_v), (w_factors, factors_v)]
+        )
+    ]
+    for copy in loads[:7]:
+        copy.start()
+
+    def pair_load(step):
+        part = pl.ds(step * chunk, chunk)
+        return pltpu.make_async_copy(pair.at[:, part], pair_v.at[:, part], pair_sems.at[step])
+
+    for step in range(depth // chunk):
+        pair_load(step).start()
+    for copy in loads[7:]:
+        copy.start()
+
+    centre, share = block_constants(wide, halves)
+    consts[0] = centre
+    consts[1] = share
+
+    def to_cols(kind, source_of, target):
+        copies = []
+        for step in range(1, col_size):
+            to = lax.rem(me_col + step, col_size)
+            copy = pltpu.make_async_remote_copy(
+                src_ref=source_of(to),
+                dst_ref=target,
+                send_sem=col_send.at[kind, step - 1],
+                recv_sem=col_recv.at[kind, step - 1],
+                device_id={"cols": to},
+                device_id_type=pl.DeviceIdType.MESH,
+            )
+            copy.start()
+            copies.append(copy)
+        return copies
+
+    owner = me_col // halves
+    mine = owner == me_row
+    half_mine = lax.rem(me_col, halves)
+
+    def fan_copies(kind, source_of, target):
+        copies = []
+        for step in range(row_size):
+            for half in range(halves):
+                to = halves * me_row + half
+                copy = pltpu.make_async_remote_copy(
+                    src_ref=source_of(half),
+                    dst_ref=target.at[me_col],
+                    send_sem=fan_send.at[kind, step * halves + half],
+                    recv_sem=fan_recv.at[kind, me_col],
+                    device_id={"rows": lax.rem(me_row + step, row_size), "cols": to},
+                    device_id_type=pl.DeviceIdType.MESH,
+                )
+                copies.append((copy, step, to))
+        return copies
+
+    def on_fan(copies, act):
+        for copy, step, to in copies:
+            if step:
+                act(copy)
+            else:
+                pl.when(to != me_col)(functools.partial(act, copy))
+
+    def fan_wait(kind, source_of, target):
+        for part in range(col_size):
+            copy = pltpu.make_async_remote_copy(
+                src_ref=source_of(0),
+                dst_ref=target.at[part],
+                send_sem=fan_send.at[kind, 0],
+                recv_sem=fan_recv.at[kind, part],
+                device_id={"rows": lax.rem(me_row + 1, row_size)},
+                device_id_type=pl.DeviceIdType.MESH,
+            )
+            pl.when(jnp.logical_not(jnp.logical_and(mine, part == me_col)))(copy.wait_recv)
+
+    loads[0].wait()
+    normed = layer_norm(single_v[...]).astype(jnp.bfloat16)
+    loads[1].wait()
+    loads[2].wait()
+    key_value = jnp.dot(
+        normed,
+        jnp.concatenate([project_v[1], project_v[2]], axis=1),
+        preferred_element_type=jnp.float32,
+    ).astype(jnp.bfloat16)
+    for half in range(halves):
+        for kind in range(2):
+            kv_send[half, kind] = key_value[
+                half * tile_cols : (half + 1) * tile_cols, kind * group : (kind + 1) * group
+            ]
+    pl.semaphore_wait(barrier, total - 1)
+    kv_copies = fan_copies(0, lambda half: kv_send.at[half], kv_recv)
+    on_fan(kv_copies, lambda copy: copy.start())
+
+    @pl.when(mine)
+    def _():
+        kv_recv[me_col] = kv_send[half_mine]
+
+    loads[3].wait()
+    loads[4].wait()
+    query_gate = jnp.dot(
+        normed,
+        jnp.concatenate([project_v[0], project_v[3]], axis=1),
+        preferred_element_type=jnp.float32,
+    )
+    q_recv[me_col] = query_gate[:, :group].astype(jnp.bfloat16)
+    q_copies = to_cols(0, lambda to: q_recv.at[me_col], q_recv.at[me_col])
+    gate_send[...] = jax.nn.sigmoid(query_gate[:, group:]).reshape(halves, depth, group)
+
+    def own_rows(to):
+        return pl.ds(pl.multiple_of(to * rows_each, rows_each), rows_each)
+
+    gate_copies = to_cols(1, lambda to: gate_send.at[:, own_rows(to)], gate_recv.at[me_col])
+    gate_recv[me_col] = gate_send[:, own_rows(me_col)]
+
+    loads[5].wait()
+    loads[6].wait()
+
+    def bias_step(step, _):
+        pair_load(step).wait()
+        parts = [
+            pair_v[half, pl.ds(step * chunk, chunk)].reshape(chunk * tile_cols, wide)
+            for half in range(halves)
+        ]
+        normed_pair = norm_centred(jnp.concatenate(parts, axis=1), consts[0], consts[1])
+        parts = [
+            normed_pair[:, half * wide : (half + 1) * wide].reshape(chunk, 1, tile_cols, wide)
+            for half in range(halves)
+        ]
+        normed_pair = jnp.concatenate(parts, axis=1).reshape(chunk * halves * tile_cols, wide)
+        bias = lax.dot_general(
+            bias_w[...], normed_pair, (((1,), (1,)), ((), ())), preferred_element_type=jnp.float32
+        )
+        bias = bias.astype(jnp.bfloat16).astype(jnp.float32)
+        for part in range(chunk):
+            bias_v[pl.ds(step * chunk + part, heads, stride=stride), :] = bias[
+                :, part * LANES : (part + 1) * LANES
+            ]
+        return 0
+
+    lax.fori_loop(0, depth // chunk, bias_step, 0)
+
+    lane_row = lane_iota((2 * halves * heads, width))
+    place = lax.broadcasted_iota(jnp.int32, (2 * halves * heads, width), 0)
+    for half in range(halves):
+        picked = jnp.where(place == half * heads + lane_row // head_width, 1.0, 0.0)
+        spread_v[half, :LANES] = picked.astype(jnp.bfloat16)
+        spread_v[half, LANES:] = picked.astype(jnp.bfloat16)
+
+    fan_wait(0, lambda half: kv_send.at[half], kv_recv)
+    for copy in q_copies:
+        copy.wait_recv()
+
+    length = jnp.sum(jnp.sum(mask_v[...], axis=1, keepdims=True), axis=0, keepdims=True)
+    lane = lane_iota((depth, LANES))
+    low = lane < tile_cols
+    valid = me_col * tile_cols + lax.rem(lane, tile_cols) < length
+    head_of = lane_iota((tile_cols, group)) // head_width
+    head_masks = [
+        jnp.where(head_of == head, 1.0, 0.0).astype(jnp.bfloat16) for head in range(heads_here)
+    ]
+    zeros = jnp.zeros((tile_cols, group), jnp.bfloat16)
+    scale = 1.0 / math.sqrt(head_width)
+    st_send[...] = jnp.zeros_like(st_send)
+    block_place = lax.broadcasted_iota(jnp.int32, (heads_here * LANES, LANES), 0) // tile_cols
+    block_target = (
+        halves * heads + lax.rem(block_place, halves) * heads + block_place // halves
+    )
+    block_lane = lane_iota((heads_here * LANES, LANES))
+
+    def attend_step(part, _):
+        query = q_recv[part]
+        query = jnp.concatenate([query[:depth], query[depth:]], axis=1)
+        key, value = kv_recv[part, 0], kv_recv[part, 1]
+        weights, value_rows = [], []
+        stats = st_send[...]
+        for first in range(0, heads_here, 2):
+            key_rows = []
+            for head in (first, first + 1):
+                masked = key * head_masks[head]
+                key_rows.append(jnp.concatenate([masked, zeros], axis=1))
+                key_rows.append(jnp.concatenate([zeros, masked], axis=1))
+            raw = lax.dot_general(
+                query,
+                jnp.concatenate(key_rows, axis=0),
+                (((1,), (1,)), ((), ())),
+                preferred_element_type=jnp.float32,
+            )
+            for head in (first, first + 1):
+                index = part * heads_here + head
+                bias = bias_v[pl.ds(pl.multiple_of(index * stride, 8), depth), :]
+                scores = raw[:, (head - first) * LANES : (head - first + 1) * LANES] * scale + bias
+                scores = jnp.where(valid, scores, excluded)
+                top0 = jnp.max(jnp.where(low, scores, excluded), axis=1, keepdims=True)
+                top1 = jnp.max(jnp.where(low, excluded, scores), axis=1, keepdims=True)
+                weights.append(
+                    jnp.exp(scores - jnp.where(low, top0, top1)).astype(jnp.bfloat16)
+                )
+                stats = jnp.where(lane == index, top0, stats)
+                stats = jnp.where(lane == heads + index, top1, stats)
+        for head in range(heads_here):
+            masked = value * head_masks[head]
+            value_rows.append(jnp.concatenate([masked, zeros], axis=1))
+            value_rows.append(jnp.concatenate([zeros, masked], axis=1))
+        weights = jnp.concatenate(weights, axis=1)
+        mixed = jnp.dot(
+            weights, jnp.concatenate(value_rows, axis=0), preferred_element_type=jnp.float32
+        )
+        ones = jnp.where(block_lane == block_target + part * heads_here, 1.0, 0.0)
+        sums = jnp.dot(weights, ones.astype(jnp.bfloat16), preferred_element_type=jnp.float32)
+        st_send[...] = stats + sums
+        pieces = [
+            mixed[:, half * group : (half + 1) * group].reshape(col_size, rows_each, group)
+            for half in range(halves)
+        ]
+        o_send[:, :, pl.ds(pl.multiple_of(part * group, group), group)] = jnp.concatenate(
+            pieces, axis=1
+        ).astype(jnp.bfloat16)
+        return 0
+
+    lax.fori_loop(0, col_size, attend_step, 0)
+
+    st_copies = to_cols(2, lambda to: st_send.at[own_rows(to)], st_recv.at[me_col])
+    o_copies = to_cols(3, lambda to: o_send.at[to], o_recv.at[me_col])
+    st_recv[me_col] = st_send[own_rows(me_col)]
+    o_recv[me_col] = o_send[me_col]
+    for copy in gate_copies + st_copies:
+        copy.wait_recv()
+    stats = st_recv[...]
+    lane = lane_iota(stats.shape)
+    top = jnp.max(stats, axis=0, keepdims=True)
+    factor = jnp.exp(stats - top)
+    sums = jnp.sum(factor * pltpu.roll(stats, halves * heads, axis=2), axis=0, keepdims=True)
+    factor = jnp.where(lane < halves * heads, factor / sums, 0.0)
+    factor = factor.reshape(col_size * rows_each, LANES)
+    high = factor.astype(jnp.bfloat16)
+    rest = (factor - high.astype(jnp.float32)).astype(jnp.bfloat16)
+    factor = jnp.concatenate([high, rest], axis=1)
+    scales = [
+        jnp.dot(factor, spread_v[half], preferred_element_type=jnp.float32) for half in range(halves)
+    ]
+    gate = jnp.concatenate(
+        [gate_recv[part].reshape(halves * rows_each, group) for part in range(col_size)], axis=1
+    )
+    for copy in o_copies:
+        copy.wait_recv()
+    attended = jnp.zeros((halves * rows_each, width), jnp.float32)
+    for part in range(col_size):
+        rows = slice(part * rows_each, (part + 1) * rows_each)
+        part_scale = jnp.concatenate([scales[half][rows] for half in range(halves)], axis=0)
+        attended = attended + part_scale * o_recv[part].astype(jnp.float32)
+    mixed = (attended * gate).astype(jnp.bfloat16)
+    for copy in loads[7:]:
+        copy.wait()
+    added = jnp.dot(mixed, out_v[...], preferred_element_type=jnp.float32)
+    own = own_single[...].astype(jnp.float32).reshape(halves * rows_each, width)
+    updated = (own + added).astype(jnp.bfloat16)
+    so_send[...] = updated.astype(jnp.float32).reshape(halves, rows_each, width).astype(jnp.bfloat16)
+    factors = jnp.dot(
+        layer_norm(updated).astype(jnp.bfloat16),
+        factors_v[...],
+        preferred_element_type=jnp.float32,
+    )
+    factors = factors.astype(jnp.bfloat16).astype(jnp.float32)
+    first, second = factors[:rows_each], factors[rows_each:]
+    shift = factors.shape[1] // 2
+    low = lane_iota(first.shape) < shift
+    left = jnp.where(low, first, pltpu.roll(second, shift, axis=1))
+    right = jnp.where(low, pltpu.roll(first, shift, axis=1), second)
+    left_send[...] = left
+    right_send[...] = right
+    right_copies = fan_copies(1, lambda half: right_send, right_recv)
+    on_fan(right_copies, lambda copy: copy.start())
+    left_copies = to_cols(4, lambda to: left_send, left_recv.at[me_col])
+    so_copies = to_cols(5, lambda to: so_send, single_out.at[:, me_col])
+    own_copy = pltpu.make_async_copy(so_send, single_out.at[:, me_col], load_sems.at[0])
+    own_copy.start()
+    left_recv[me_col] = left
+
+    @pl.when(mine)
+    def _():
+        right_recv[me_col] = right_send[...]
+
+    fan_wait(1, lambda half: right_send, right_recv)
+    for copy in left_copies:
+        copy.wait_recv()
+    left = left_recv[...].reshape(depth, LANES)
+    turned = pltpu.roll(left, shift, axis=1)
+    low = lane_iota(left.shape) < shift
+    left_out[:depth] = jnp.where(low, left, turned)
+    left_out[depth:] = jnp.where(low, turned, left)
+    right = right_recv[...].reshape(tile_cols, LANES)
+    turned = pltpu.roll(right, shift, axis=1)
+    right_out[...] = jnp.where(lane_iota(right.shape) // shift == half_mine, right, turned)
+
+    for copies in (q_copies, gate_copies, st_copies, o_copies, left_copies, so_copies):
+        for copy in copies:
+            copy.wait_send()
+    on_fan(kv_copies, lambda copy: copy.wait_send())
+    on_fan(right_copies, lambda copy: copy.wait_send())
+    for copy in so_copies:
+        copy.wait_recv()
+    own_copy.wait()
+
+
+def attend(single, pair, mask, w_bias, w_project, w_out, w_factors, row_size, col_size):
+    tile_rows, tile_cols, wide = pair.shape
+    width = single.shape[1]
+    heads = w_bias.shape[1]
+    halves = tile_rows // tile_cols
+    depth = tile_rows // halves
+    rows_each = depth // col_size
+    group = w_project.shape[2]
+    steps = 8
+    stride = depth + 8
+    any_spec = pl.BlockSpec(memory_space=pl.ANY)
+    vmem_spec = pl.BlockSpec(memory_space=pltpu.VMEM)
+    bf16, f32 = jnp.bfloat16, jnp.float32
+    single_out, left, right = pl.pallas_call(
+        functools.partial(attend_kernel, row_size, col_size, heads, tile_cols, stride),
+        out_shape=(
+            jax.ShapeDtypeStruct((halves, col_size, rows_each, width), bf16),
+            jax.ShapeDtypeStruct((tile_rows, wide), f32),
+            jax.ShapeDtypeStruct((tile_cols, wide), f32),
+        ),
+        in_specs=[any_spec] * 7,
+        out_specs=[any_spec, vmem_spec, vmem_spec],
+        scratch_shapes=[
+            pltpu.VMEM((tile_rows, width), bf16),
+            pltpu.VMEM((halves, depth, tile_cols, wide), bf16),
+            pltpu.VMEM((mask.shape[0] // LANES, LANES), jnp.int32),
+            pltpu.VMEM((heads, wide), bf16),
+            pltpu.VMEM(w_project.shape, bf16),
+            pltpu.VMEM(w_out.shape, bf16),
+            pltpu.VMEM(w_factors.shape, bf16),
+            pltpu.VMEM((halves, rows_each, width), bf16),
+            pltpu.VMEM((halves, 2, tile_cols, group), bf16),
+            pltpu.VMEM((col_size, 2, tile_cols, group), bf16),
+            pltpu.VMEM((col_size, tile_rows, group), bf16),
+            pltpu.VMEM((halves, depth, group), f32),
+            pltpu.VMEM((col_size, halves, rows_each, group), f32),
+            pltpu.VMEM((heads * stride, LANES), f32),
+            pltpu.VMEM((col_size, halves * rows_each, width), bf16),
+            pltpu.VMEM((col_size, halves * rows_each, width), bf16),
+            pltpu.VMEM((depth, LANES), f32),
+            pltpu.VMEM((col_size, rows_each, LANES), f32),
+            pltpu.VMEM((rows_each, LANES), f32),
+            pltpu.VMEM((rows_each, LANES), f32),
+            pltpu.VMEM((col_size, rows_each, LANES), f32),
+            pltpu.VMEM((col_size, rows_each, LANES), f32),
+            pltpu.VMEM((halves, rows_each, width), bf16),
+            pltpu.VMEM((2, halves * wide, halves * wide), bf16),
+            pltpu.VMEM((halves, 2 * LANES, width), bf16),
+            pltpu.SemaphoreType.DMA((9 + halves,)),
+            pltpu.SemaphoreType.DMA((steps,)),
+            pltpu.SemaphoreType.DMA((6, col_size - 1)),
+            pltpu.SemaphoreType.DMA((6, col_size - 1)),
+            pltpu.SemaphoreType.DMA((2, row_size * halves)),
+            pltpu.SemaphoreType.DMA((2, col_size)),
+        ],
+        compiler_params=pltpu.CompilerParams(collective_id=3, has_side_effects=True),
+        name="attend",
+    )(
+        single,
+        pair.reshape(halves, depth, tile_cols, wide),
+        mask.reshape(mask.shape[0] // LANES, LANES),
+        w_bias.T,
+        w_project,
+        w_out,
+        w_factors,
+    )
+    return single_out.reshape(tile_rows, width), left, right
+
+
+def fits(row_size, col_size, single, pair, mask, w_bias, w_project, w_factors):
+    tile_rows, tile_cols, wide = pair.shape
+    heads = w_bias.shape[1]
+    return (
+        tile_rows == 2 * tile_cols
+        and 2 * tile_cols == LANES
+        and wide == LANES
+        and w_factors.shape[1] == LANES
+        and w_project.shape[2] == LANES
+        and 4 * heads == LANES
+        and heads % (2 * col_size) == 0
+        and tile_cols % (8 * col_size) == 0
+        and col_size == 2 * row_size
+        and mask.shape[0] % LANES == 0
+    )
+
+
+def per_device_keys(
+    row_size, col_size,
+    single, pair, residue_mask, w_bias, w_project, w_out, w_factors, w_pairout, w_up, w_down
+):
+    single_out, left, right = attend(
+        single, pair, residue_mask, w_bias, w_project, w_out, w_factors, row_size, col_size
+    )
+    return (single_out, update_pair(pair, left, right, w_pairout, w_up, w_down))
+
+
+def dispatch(row_size, col_size, *arrays):
+    single, pair, residue_mask, w_bias, w_project, w_out, w_factors = arrays[:7]
+    if fits(row_size, col_size, single, pair, residue_mask, w_bias, w_project, w_factors):
+        return per_device_keys(row_size, col_size, *arrays)
+    return per_device(row_size, col_size, *arrays)
+
+
 def solution(mesh):
     return jax.shard_map(
-        functools.partial(per_device, mesh.shape["rows"], mesh.shape["cols"]),
+        functools.partial(dispatch, mesh.shape["rows"], mesh.shape["cols"]),
         mesh=mesh,
         in_specs=(
             P("rows", None),

time: 62.5 us -> 65.2 us (1.043)
  Pallas kernels: 38.3 us -> 63.7 us
  starting transfers between devices: 7.28 us -> 0 us
  matrix products: 4.99 us -> 0 us
  waiting for transfers between devices: 4.27 us -> 0 us
  local copies, waits for them, and re-layouts: 4.25 us -> 0.71 us
  other arithmetic: 2.08 us -> 0 us
    pallas_call x3 -> x1, Pallas kernels: 27.2 us -> 52.6 us  [attend(): pl.pallas_call(functools.partial(attend_kernel, row_size, col_size, heads...]
    all_to_all x1 -> x0, starting transfers between devices: 7.28 us -> none  [per_device(): lax.all_to_all(bias_local, 'cols', split_axis=0, concat_axis=2, tiled=True)]
    dot_general x3 -> x0, matrix products: 4.47 us -> none  [the longest x1 3.08 us: per_device(): jnp.einsum('rcp,ph->hrc', normed_pair, w_bias, preferred_element_type=jnp...]
    all_to_all x1 -> x0, waiting for transfers between devices: 4.27 us -> none  [per_device(): lax.all_to_all(bias_local, 'cols', split_axis=0, concat_axis=2, tiled=True)]
    convert_element_type x3 -> x0, local copies, waits for them, and re-layouts: 1.4 us -> none  [the longest x1 1 us: per_device(): bias_local = jnp.einsum('rcp,ph->hrc', normed_pair, w_bias, preferred_ele...]
    slice x5 -> x0, local copies, waits for them, and re-layouts: 1.35 us -> none  [the longest x2 1.1 us: per_device(): both[:, :key_local.shape[1]]]
    convert_element_type x2 -> x0, other arithmetic: 0.75 us -> none  [the longest x1 0.65 us: per_device(): mixed = (attended * gate_values).astype(jnp.bfloat16)]
  transfers between devices with their start and end apart: 1 -> 0, of which waited for: 1 -> 0; matrix products, arithmetic and copies ran while one was open for 6% -> 0% of each run, Pallas kernels for 11% -> 0%
where the time goes in v1:
time: 65.2 us; the launch traced here: 65.1 us
  Pallas kernels  63.7 us (98%)
  local copies, waits for them, and re-layouts  0.71 us (1%)
    pallas_call x1, Pallas kernels, attend(): pl.pallas_call(functools.partial(attend_kernel, row_size, col_size, heads...  52.6 us
    pallas_call x1, Pallas kernels, update_pair(): pl.pallas_call(pair_kernel, out_shape=jax.ShapeDtypeStruct(pair.shape, jn...  11.1 us

profile of v1, /device:TPU:0, one launch (start us, length us, event | category | flops | bytes accessed | tf_op | source)
XLA Modules:
  0.0 65.1 jit_solution(15433515244513595375)
XLA Ops:
  0.6 52.6 %attend.1 = (bf16[2,8,8,1024]{3,2,1,0:T(8,128)(2,1)}, f32[128,128]{1,0:T(8,128)}, f32[64,128]{1,0:T(8,128)}) custom-call(bf16[128,1024]{1,0:T(8,128)(2,1)} %single.1, bf16[2,64,64,128]{3,2,1,0:T(8,128)(2,1)} %bitcast.4, s32[4,128]{1,0:T(4,128)} %bitcast.7, bf16[32,128]{1,0:T(8,128)(2,1)} %bitcast.6, bf16[4,1024,128]{2,1,0:T(8,128)(2,1)} %w_project.1, ...), custom_call_target="tpu_custom_call" | custom-call | tf_op jit(solution)/shard_map/attend/pallas_call | solution.py:672
  53.3 0.0 copy-start
  53.3 11.1 %update_pair.1 = bf16[128,64,128]{2,1,0:T(8,128)(2,1)} custom-call(bf16[128,64,128]{2,1,0:T(8,128)(2,1)} %pair.1, f32[128,128]{1,0:T(8,128)} %get-tuple-element.6.left, f32[64,128]{1,0:T(8,128)} %get-tuple-element.7.right, bf16[128,128]{1,0:T(8,128)(2,1)} %w_pairout.1, bf16[128,512]{1,0:T(8,128)(2,1)} %w_up.1, bf16[512,128]{1,0:T(8,128)(2,1)} %w_down.1), custom_call_target="tpu_custom_call" | custom-call | tf_op jit(solution)/shard_map/update_pair/pallas_call | solution.py:220
  64.4 0.0 copy-done
  64.4 0.7 %copy.13 = bf16[128,1024]{1,0:T(8,128)(2,1)} copy(bf16[128,1024]{1,0:T(8,128)(2,1)S(1)} %bitcast.5) | data formatting | bytes 524288
Async XLA Ops:
  53.3 11.1 %copy-start = (bf16[2,8,8,1024]{3,2,1,0:T(8,128)(2,1)S(1)}, bf16[2,8,8,1024]{3,2,1,0:T(8,128)(2,1)}, u32[]{:S(2)}) copy-start(bf16[2,8,8,1024]{3,2,1,0:T(8,128)(2,1)} %get-tuple-element.5) | copy-start | bytes 786436

commit v2 on v1

--- a/solution.py
+++ b/solution.py
@@ -322,6 +322,7 @@
     kv_send, kv_recv, q_recv, gate_send, gate_recv, bias_v, o_send, o_recv,
     st_send, st_recv, left_send, right_send, left_recv, right_recv, so_send, consts, spread_v,
     load_sems, pair_sems, col_send, col_recv, fan_send, fan_recv,
+    kv_sent, kv_came, kv_relayed, q_sent, q_came, o_sent, o_came,
 ):
     me_row = lax.axis_index("rows")
     me_col = lax.axis_index("cols")
@@ -408,6 +409,37 @@
                 copies.append((copy, step, to))
         return copies
 
+    def on_some(copies, act):
+        for copy, condition in copies:
+            if condition is None:
+                act(copy)
+            else:
+                pl.when(condition)(functools.partial(act, copy))
+
+    kind_mine = lax.rem(me_row, 2)
+    row_mate = me_row + 1 - 2 * kind_mine
+    col_mate = me_col + 1 - 2 * lax.rem(me_col, 2)
+
+    def relay_keys(part, kind, slot):
+        return pltpu.make_async_remote_copy(
+            src_ref=kv_recv.at[part, kind],
+            dst_ref=kv_recv.at[part, kind],
+            send_sem=kv_relayed.at[slot],
+            recv_sem=kv_came.at[kind, part],
+            device_id={"rows": row_mate},
+            device_id_type=pl.DeviceIdType.MESH,
+        )
+
+    def send_query(part, to, slot):
+        return pltpu.make_async_remote_copy(
+            src_ref=q_recv.at[part],
+            dst_ref=q_recv.at[part],
+            send_sem=q_sent.at[slot],
+            recv_sem=q_came.at[part],
+            device_id={"cols": to},
+            device_id_type=pl.DeviceIdType.MESH,
+        )
+
     def on_fan(copies, act):
         for copy, step, to in copies:
             if step:
@@ -442,12 +474,28 @@
                 half * tile_cols : (half + 1) * tile_cols, kind * group : (kind + 1) * group
             ]
     pl.semaphore_wait(barrier, total - 1)
-    kv_copies = fan_copies(0, lambda half: kv_send.at[half], kv_recv)
-    on_fan(kv_copies, lambda copy: copy.start())
+    kv_copies = []
+    for step in range(row_size // 2):
+        for kind in range(2):
+            for half in range(halves):
+                to = halves * me_row + half
+                row = 2 * lax.rem(me_row // 2 + step, row_size // 2) + kind
+                copy = pltpu.make_async_remote_copy(
+                    src_ref=kv_send.at[half, kind],
+                    dst_ref=kv_recv.at[me_col, kind],
+                    send_sem=kv_sent.at[(step * 2 + kind) * halves + half],
+                    recv_sem=kv_came.at[kind, me_col],
+                    device_id={"rows": row, "cols": to},
+                    device_id_type=pl.DeviceIdType.MESH,
+                )
+                here = jnp.logical_and(row == me_row, to == me_col)
+                copies_of = (copy, None if step else jnp.logical_not(here))
+                kv_copies.append(copies_of)
+    on_some(kv_copies, lambda copy: copy.start())
 
     @pl.when(mine)
     def _():
-        kv_recv[me_col] = kv_send[half_mine]
+        kv_recv[me_col, kind_mine] = kv_send[half_mine, kind_mine]
 
     loads[3].wait()
     loads[4].wait()
@@ -457,7 +505,12 @@
         preferred_element_type=jnp.float32,
     )
     q_recv[me_col] = query_gate[:, :group].astype(jnp.bfloat16)
-    q_copies = to_cols(0, lambda to: q_recv.at[me_col], q_recv.at[me_col])
+    peers = [lax.rem(me_col + 2 * step, col_size) for step in range(1, col_size // 2)]
+    mates = [lax.rem(col_mate + 2 * step, col_size) for step in range(1, col_size // 2)]
+    q_copies = [send_query(me_col, to, slot) for slot, to in enumerate(peers)]
+    q_copies.append(send_query(me_col, col_mate, len(peers)))
+    for copy in q_copies:
+        copy.start()
     gate_send[...] = jax.nn.sigmoid(query_gate[:, group:]).reshape(halves, depth, group)
 
     def own_rows(to):
@@ -500,9 +553,21 @@
         spread_v[half, :LANES] = picked.astype(jnp.bfloat16)
         spread_v[half, LANES:] = picked.astype(jnp.bfloat16)
 
-    fan_wait(0, lambda half: kv_send.at[half], kv_recv)
-    for copy in q_copies:
+    relays = []
+    for part in range(col_size):
+        copy = relay_keys(part, kind_mine, part)
+        pl.when(jnp.logical_not(jnp.logical_and(mine, part == me_col)))(copy.wait_recv)
+        copy.start()
+        relays.append(copy)
+    for slot, peer in enumerate(peers):
+        copy = send_query(peer, col_mate, col_size // 2 + slot)
         copy.wait_recv()
+        copy.start()
+        relays.append(copy)
+    for part in range(col_size):
+        relay_keys(part, 1 - kind_mine, part).wait_recv()
+    for part in [col_mate] + mates:
+        send_query(part, col_mate, 0).wait_recv()
 
     length = jnp.sum(jnp.sum(mask_v[...], axis=1, keepdims=True), axis=0, keepdims=True)
     lane = lane_iota((depth, LANES))
@@ -521,7 +586,7 @@
     )
     block_lane = lane_iota((heads_here * LANES, LANES))
 
-    def attend_step(part, _):
+    def attend_part(part):
         query = q_recv[part]
         query = jnp.concatenate([query[:depth], query[depth:]], axis=1)
         key, value = kv_recv[part, 0], kv_recv[part, 1]
@@ -566,17 +631,38 @@
             mixed[:, half * group : (half + 1) * group].reshape(col_size, rows_each, group)
             for half in range(halves)
         ]
-        o_send[:, :, pl.ds(pl.multiple_of(part * group, group), group)] = jnp.concatenate(
-            pieces, axis=1
-        ).astype(jnp.bfloat16)
+        return jnp.concatenate(pieces, axis=1).astype(jnp.bfloat16)
+
+    parts, _, _, part_width = o_send.shape
+    each = part_width // group
+
+    def o_copy(step, shift):
+        to = lax.rem(me_col + shift, col_size)
+        return pltpu.make_async_remote_copy(
+            src_ref=o_send.at[step, to],
+            dst_ref=o_recv.at[step, me_col],
+            send_sem=o_sent.at[step, shift - 1],
+            recv_sem=o_came.at[step, shift - 1],
+            device_id={"cols": to},
+            device_id_type=pl.DeviceIdType.MESH,
+        )
+
+    def attend_step(step, _):
+        for index in range(each):
+            o_send[step, :, :, index * group : (index + 1) * group] = attend_part(
+                step * each + index
+            )
+        for shift in range(1, col_size):
+            o_copy(step, shift).start()
         return 0
 
-    lax.fori_loop(0, col_size, attend_step, 0)
+    lax.fori_loop(0, parts, attend_step, 0)
 
     st_copies = to_cols(2, lambda to: st_send.at[own_rows(to)], st_recv.at[me_col])
-    o_copies = to_cols(3, lambda to: o_send.at[to], o_recv.at[me_col])
     st_recv[me_col] = st_send[own_rows(me_col)]
-    o_recv[me_col] = o_send[me_col]
+    for step in range(parts):
+        o_recv[step, me_col] = o_send[step, me_col]
+    o_copies = [o_copy(step, shift) for step in range(parts) for shift in range(1, col_size)]
     for copy in gate_copies + st_copies:
         copy.wait_recv()
     stats = st_recv[...]
@@ -601,7 +687,8 @@
     for part in range(col_size):
         rows = slice(part * rows_each, (part + 1) * rows_each)
         part_scale = jnp.concatenate([scales[half][rows] for half in range(halves)], axis=0)
-        attended = attended + part_scale * o_recv[part].astype(jnp.float32)
+        whole = jnp.concatenate([o_recv[step, part] for step in range(parts)], axis=1)
+        attended = attended + part_scale * whole.astype(jnp.float32)
     mixed = (attended * gate).astype(jnp.bfloat16)
     for copy in loads[7:]:
         copy.wait()
@@ -646,10 +733,10 @@
     turned = pltpu.roll(right, shift, axis=1)
     right_out[...] = jnp.where(lane_iota(right.shape) // shift == half_mine, right, turned)
 
-    for copies in (q_copies, gate_copies, st_copies, o_copies, left_copies, so_copies):
+    for copies in (q_copies, relays, gate_copies, st_copies, o_copies, left_copies, so_copies):
         for copy in copies:
             copy.wait_send()
-    on_fan(kv_copies, lambda copy: copy.wait_send())
+    on_some(kv_copies, lambda copy: copy.wait_send())
     on_fan(right_copies, lambda copy: copy.wait_send())
     for copy in so_copies:
         copy.wait_recv()
@@ -665,6 +752,7 @@
     rows_each = depth // col_size
     group = w_project.shape[2]
     steps = 8
+    parts = col_size // 2
     stride = depth + 8
     any_spec = pl.BlockSpec(memory_space=pl.ANY)
     vmem_spec = pl.BlockSpec(memory_space=pltpu.VMEM)
@@ -693,8 +781,8 @@
             pltpu.VMEM((halves, depth, group), f32),
             pltpu.VMEM((col_size, halves, rows_each, group), f32),
             pltpu.VMEM((heads * stride, LANES), f32),
-            pltpu.VMEM((col_size, halves * rows_each, width), bf16),
-            pltpu.VMEM((col_size, halves * rows_each, width), bf16),
+            pltpu.VMEM((parts, col_size, halves * rows_each, width // parts), bf16),
+            pltpu.VMEM((parts, col_size, halves * rows_each, width // parts), bf16),
             pltpu.VMEM((depth, LANES), f32),
             pltpu.VMEM((col_size, rows_each, LANES), f32),
             pltpu.VMEM((rows_each, LANES), f32),
@@ -710,6 +798,13 @@
             pltpu.SemaphoreType.DMA((6, col_size - 1)),
             pltpu.SemaphoreType.DMA((2, row_size * halves)),
             pltpu.SemaphoreType.DMA((2, col_size)),
+            pltpu.SemaphoreType.DMA((row_size * halves,)),
+            pltpu.SemaphoreType.DMA((2, col_size)),
+            pltpu.SemaphoreType.DMA((col_size,)),
+            pltpu.SemaphoreType.DMA((col_size,)),
+            pltpu.SemaphoreType.DMA((col_size,)),
+            pltpu.SemaphoreType.DMA((parts, col_size - 1)),
+            pltpu.SemaphoreType.DMA((parts, col_size - 1)),
         ],
         compiler_params=pltpu.CompilerParams(collective_id=3, has_side_effects=True),
         name="attend",
@@ -738,6 +833,7 @@
         and heads % (2 * col_size) == 0
         and tile_cols % (8 * col_size) == 0
         and col_size == 2 * row_size
+        and row_size % 2 == 0
         and mask.shape[0] % LANES == 0
     )
 

time: 65.2 us -> 55.3 us (0.85)
  Pallas kernels: 63.7 us -> 53.8 us
    pallas_call x1, Pallas kernels: 52.6 us -> 42.6 us  [attend(): pl.pallas_call(functools.partial(attend_kernel, row_size, col_size, heads...]
where the time goes in v2:
time: 55.3 us; the launch traced here: 55.1 us
  Pallas kernels  53.8 us (97%)
  local copies, waits for them, and re-layouts  0.71 us (1%)
  between operations  0.65 us (1%)
    pallas_call x1, Pallas kernels, attend(): pl.pallas_call(functools.partial(attend_kernel, row_size, col_size, heads...  42.6 us
    pallas_call x1, Pallas kernels, update_pair(): pl.pallas_call(pair_kernel, out_shape=jax.ShapeDtypeStruct(pair.shape, jn...  11.1 us

profile of v2, /device:TPU:0, one launch (start us, length us, event | category | flops | bytes accessed | tf_op | source)
XLA Modules:
  0.0 55.1 jit_solution(11586758457881086713)
XLA Ops:
  0.6 42.6 %attend.1 = (bf16[2,8,8,1024]{3,2,1,0:T(8,128)(2,1)}, f32[128,128]{1,0:T(8,128)}, f32[64,128]{1,0:T(8,128)}) custom-call(bf16[128,1024]{1,0:T(8,128)(2,1)} %single.1, bf16[2,64,64,128]{3,2,1,0:T(8,128)(2,1)} %bitcast.4, s32[4,128]{1,0:T(4,128)} %bitcast.7, bf16[32,128]{1,0:T(8,128)(2,1)} %bitcast.6, bf16[4,1024,128]{2,1,0:T(8,128)(2,1)} %w_project.1, ...), custom_call_target="tpu_custom_call" | custom-call | tf_op jit(solution)/shard_map/attend/pallas_call | solution.py:760
  43.3 0.0 copy-start
  43.3 11.1 %update_pair.1 = bf16[128,64,128]{2,1,0:T(8,128)(2,1)} custom-call(bf16[128,64,128]{2,1,0:T(8,128)(2,1)} %pair.1, f32[128,128]{1,0:T(8,128)} %get-tuple-element.6.left, f32[64,128]{1,0:T(8,128)} %get-tuple-element.7.right, bf16[128,128]{1,0:T(8,128)(2,1)} %w_pairout.1, bf16[128,512]{1,0:T(8,128)(2,1)} %w_up.1, bf16[512,128]{1,0:T(8,128)(2,1)} %w_down.1), custom_call_target="tpu_custom_call" | custom-call | tf_op jit(solution)/shard_map/update_pair/pallas_call | solution.py:220
  54.4 0.0 copy-done
  54.4 0.7 %copy.13 = bf16[128,1024]{1,0:T(8,128)(2,1)} copy(bf16[128,1024]{1,0:T(8,128)(2,1)S(1)} %bitcast.5) | data formatting | bytes 524288
Async XLA Ops:
  43.3 11.1 %copy-start = (bf16[2,8,8,1024]{3,2,1,0:T(8,128)(2,1)S(1)}, bf16[2,8,8,1024]{3,2,1,0:T(8,128)(2,1)}, u32[]{:S(2)}) copy-start(bf16[2,8,8,1024]{3,2,1,0:T(8,128)(2,1)} %get-tuple-element.5) | copy-start | bytes 786436

commit v3 on v2

--- a/solution.py
+++ b/solution.py
@@ -288,39 +288,71 @@
 
 LANES = 128
 excluded = -1e30
+update_block = 16
 
 
 def lane_iota(shape):
     return lax.broadcasted_iota(jnp.int32, shape, len(shape) - 1)
 
 
-def block_constants(wide, copies):
+def centre_matrix(wide, copies):
     size = wide * copies
     row = lax.broadcasted_iota(jnp.int32, (size, size), 0)
     col = lax.broadcasted_iota(jnp.int32, (size, size), 1)
-    same = row // wide == col // wide
-    share = jnp.where(same, 1.0 / wide, 0.0)
-    centre = jnp.where(row == col, 1.0, 0.0) - share
-    return centre.astype(jnp.bfloat16), share.astype(jnp.bfloat16)
-
-
-def norm_centred(values, centre, share):
+    share = jnp.where(row // wide == col // wide, 1.0 / wide, 0.0)
+    return (jnp.where(row == col, 1.0, 0.0) - share).astype(jnp.bfloat16)
+
+
+def norm_centred(values, centre, copies):
     centred = jnp.dot(values, centre, preferred_element_type=jnp.float32)
-    square = centred * centred
-    high = square.astype(jnp.bfloat16)
-    low = (square - high.astype(jnp.float32)).astype(jnp.bfloat16)
-    spread_out = jnp.dot(high, share, preferred_element_type=jnp.float32)
-    spread_out = spread_out + jnp.dot(low, share, preferred_element_type=jnp.float32)
-    return (centred * lax.rsqrt(spread_out + epsilon)).astype(jnp.bfloat16)
+    wide = values.shape[1] // copies
+    parts = []
+    for index in range(copies):
+        part = centred[:, index * wide : (index + 1) * wide]
+        square = jnp.sum(part * part, axis=1, keepdims=True) * (1.0 / wide)
+        parts.append((part * lax.rsqrt(square + epsilon)).astype(jnp.bfloat16))
+    return parts
+
+
+def twice(weights):
+    zeros = jnp.zeros_like(weights)
+    upper = jnp.concatenate([weights, zeros], axis=1)
+    return jnp.concatenate([upper, jnp.concatenate([zeros, weights], axis=1)], axis=0)
+
+
+def update_rows(pair_of, left_of, right, rows, centre, w_pairout, w_up, w_down):
+    tile_cols, wide = right.shape
+    lower = lane_iota((rows, tile_cols, wide)) < wide // 2
+
+    def paired(index):
+        left_wide = left_of(index)[:, None, :]
+        right_wide = right[None, :, :]
+        chosen = jnp.where(lower, left_wide * right_wide, left_wide - right_wide)
+        return chosen.astype(jnp.bfloat16).reshape(rows * tile_cols, wide)
+
+    flat = [pair_of(index).reshape(rows * tile_cols, wide) for index in range(2)]
+    mid = jnp.concatenate(flat, axis=1).astype(jnp.float32) + jnp.dot(
+        jnp.concatenate([paired(0), paired(1)], axis=1),
+        w_pairout,
+        preferred_element_type=jnp.float32,
+    )
+    mid = mid.astype(jnp.bfloat16)
+    normed = jnp.concatenate(norm_centred(mid, centre, 2), axis=0)
+    mid = jnp.concatenate([mid[:, :wide], mid[:, wide:]], axis=0)
+    hidden = jnp.dot(normed, w_up, preferred_element_type=jnp.float32)
+    hidden = jnp.maximum(hidden, 0.0).astype(jnp.bfloat16)
+    out = mid.astype(jnp.float32) + jnp.dot(hidden, w_down, preferred_element_type=jnp.float32)
+    return out.astype(jnp.bfloat16).reshape(2 * rows, tile_cols, wide)
 
 
 def attend_kernel(
     row_size, col_size, heads, tile_cols, stride,
-    single, pair, mask, w_bias, w_project, w_out, w_factors,
-    single_out, left_out, right_out,
+    single, pair, mask, w_bias, w_project, w_out, w_factors, w_pairout, w_up, w_down,
+    single_out, left_out, right_out, part_out,
     single_v, pair_v, mask_v, bias_w, project_v, out_v, factors_v, own_single,
     kv_send, kv_recv, q_recv, gate_send, gate_recv, bias_v, o_send, o_recv,
-    st_send, st_recv, left_send, right_send, left_recv, right_recv, so_send, consts, spread_v,
+    st_send, st_recv, left_send, right_send, left_recv, right_recv, so_send, centre_v, spread_v,
+    pairout_v, twice_v, up_v, down_v, part_v,
     load_sems, pair_sems, col_send, col_recv, fan_send, fan_recv,
     kv_sent, kv_came, kv_relayed, q_sent, q_came, o_sent, o_came,
 ):
@@ -355,6 +387,7 @@
                 for half in range(halves)
             ]
             + [(w_out, out_v), (w_factors, factors_v)]
+            + [(w_pairout, pairout_v), (w_up, up_v), (w_down, down_v)]
         )
     ]
     for copy in loads[:7]:
@@ -369,9 +402,7 @@
     for copy in loads[7:]:
         copy.start()
 
-    centre, share = block_constants(wide, halves)
-    consts[0] = centre
-    consts[1] = share
+    centre_v[...] = centre_matrix(wide, halves)
 
     def to_cols(kind, source_of, target):
         copies = []
@@ -516,9 +547,6 @@
     def own_rows(to):
         return pl.ds(pl.multiple_of(to * rows_each, rows_each), rows_each)
 
-    gate_copies = to_cols(1, lambda to: gate_send.at[:, own_rows(to)], gate_recv.at[me_col])
-    gate_recv[me_col] = gate_send[:, own_rows(me_col)]
-
     loads[5].wait()
     loads[6].wait()
 
@@ -528,11 +556,8 @@
             pair_v[half, pl.ds(step * chunk, chunk)].reshape(chunk * tile_cols, wide)
             for half in range(halves)
         ]
-        normed_pair = norm_centred(jnp.concatenate(parts, axis=1), consts[0], consts[1])
-        parts = [
-            normed_pair[:, half * wide : (half + 1) * wide].reshape(chunk, 1, tile_cols, wide)
-            for half in range(halves)
-        ]
+        parts = norm_centred(jnp.concatenate(parts, axis=1), centre_v[...], halves)
+        parts = [part.reshape(chunk, 1, tile_cols, wide) for part in parts]
         normed_pair = jnp.concatenate(parts, axis=1).reshape(chunk * halves * tile_cols, wide)
         bias = lax.dot_general(
             bias_w[...], normed_pair, (((1,), (1,)), ((), ())), preferred_element_type=jnp.float32
@@ -568,6 +593,8 @@
         relay_keys(part, 1 - kind_mine, part).wait_recv()
     for part in [col_mate] + mates:
         send_query(part, col_mate, 0).wait_recv()
+    gate_copies = to_cols(1, lambda to: gate_send.at[:, own_rows(to)], gate_recv.at[me_col])
+    gate_recv[me_col] = gate_send[:, own_rows(me_col)]
 
     length = jnp.sum(jnp.sum(mask_v[...], axis=1, keepdims=True), axis=0, keepdims=True)
     lane = lane_iota((depth, LANES))
@@ -733,6 +760,31 @@
     turned = pltpu.roll(right, shift, axis=1)
     right_out[...] = jnp.where(lane_iota(right.shape) // shift == half_mine, right, turned)
 
+    twice_v[...] = twice(pairout_v[...])
+    block = update_block
+    starts = depth // (2 * block)
+
+    def part_copy(step):
+        rows = pl.ds(step * 2 * block, 2 * block)
+        return pltpu.make_async_copy(part_v.at[rows], part_out.at[rows], pair_sems.at[step])
+
+    def update_step(step, _):
+        first = step * 2 * block
+        part_v[pl.ds(first, 2 * block)] = update_rows(
+            lambda index: pair_v[0, pl.ds(first + index * block, block)],
+            lambda index: left_out[pl.ds(pl.multiple_of(first + index * block, 8), block)],
+            right_out[...],
+            block,
+            centre_v[...],
+            twice_v[...],
+            up_v[...],
+            down_v[...],
+        )
+        part_copy(step).start()
+        return 0
+
+    lax.fori_loop(0, starts, update_step, 0)
+
     for copies in (q_copies, relays, gate_copies, st_copies, o_copies, left_copies, so_copies):
         for copy in copies:
             copy.wait_send()
@@ -741,31 +793,119 @@
     for copy in so_copies:
         copy.wait_recv()
     own_copy.wait()
-
-
-def attend(single, pair, mask, w_bias, w_project, w_out, w_factors, row_size, col_size):
-    tile_rows, tile_cols, wide = pair.shape
-    width = single.shape[1]
+    for step in range(starts):
+        part_copy(step).wait()
+
+
+def finish_kernel(
+    single, pair, part, left, right, w_pairout, w_up, w_down,
+    single_out, pair_out,
+    single_v, pair_v, part_v, done_v, centre_v, twice_v, sems, out_sems,
+):
+    _, depth, tile_cols, wide = pair.shape
+    block = update_block
+    steps = depth // (2 * block)
+
+    def rows(step):
+        return pl.ds(step * 2 * block, 2 * block)
+
+    loads = [
+        pltpu.make_async_copy(pair.at[1, rows(step)], pair_v.at[rows(step)], sems.at[2 + step])
+        for step in range(steps)
+    ]
+    through = [
+        (pltpu.make_async_copy(part, part_v, sems.at[0]),
+         pltpu.make_async_copy(part_v, pair_out.at[0], out_sems.at[0])),
+        (pltpu.make_async_copy(single, single_v, sems.at[1]),
+         pltpu.make_async_copy(single_v, single_out, out_sems.at[1])),
+    ]
+    for copy in loads:
+        copy.start()
+    for copy, _ in through:
+        copy.start()
+    centre_v[...] = centre_matrix(wide, 2)
+    twice_v[...] = twice(w_pairout[...])
+    stores = []
+    for step in range(steps):
+        loads[step].wait()
+        first = step * 2 * block
+        done_v[rows(step)] = update_rows(
+            lambda index: pair_v[first + index * block : first + (index + 1) * block],
+            lambda index: left[depth + first + index * block : depth + first + (index + 1) * block],
+            right[...],
+            block,
+            centre_v[...],
+            twice_v[...],
+            w_up[...],
+            w_down[...],
+        )
+        store = pltpu.make_async_copy(
+            done_v.at[rows(step)], pair_out.at[1, rows(step)], out_sems.at[2 + step]
+        )
+        store.start()
+        stores.append(store)
+        if step == 0:
+            for load, later in through:
+                load.wait()
+                later.start()
+                stores.append(later)
+    for store in stores:
+        store.wait()
+
+
+def finish(single, pair, part, left, right, w_pairout, w_up, w_down):
+    halves, depth, tile_cols, wide = pair.shape
+    steps = depth // (2 * update_block)
+    any_spec = pl.BlockSpec(memory_space=pl.ANY)
+    vmem_spec = pl.BlockSpec(memory_space=pltpu.VMEM)
+    bf16 = jnp.bfloat16
+    return pl.pallas_call(
+        finish_kernel,
+        out_shape=(
+            jax.ShapeDtypeStruct(single.shape, bf16),
+            jax.ShapeDtypeStruct(pair.shape, bf16),
+        ),
+        in_specs=[any_spec] * 3 + [vmem_spec] * 5,
+        out_specs=[any_spec] * 2,
+        scratch_shapes=[
+            pltpu.VMEM(single.shape, bf16),
+            pltpu.VMEM((depth, tile_cols, wide), bf16),
+            pltpu.VMEM((depth, tile_cols, wide), bf16),
+            pltpu.VMEM((depth, tile_cols, wide), bf16),
+            pltpu.VMEM((2 * wide, 2 * wide), bf16),
+            pltpu.VMEM((2 * wide, 2 * wide), bf16),
+            pltpu.SemaphoreType.DMA((2 + steps,)),
+            pltpu.SemaphoreType.DMA((2 + steps,)),
+        ],
+        name="finish",
+    )(single, pair, part, left, right, w_pairout, w_up, w_down)
+
+
+def attend(
+    single, pair, mask, w_bias, w_project, w_out, w_factors, w_pairout, w_up, w_down,
+    row_size, col_size,
+):
+    halves, depth, tile_cols, wide = pair.shape
+    tile_rows, width = single.shape
     heads = w_bias.shape[1]
-    halves = tile_rows // tile_cols
-    depth = tile_rows // halves
     rows_each = depth // col_size
     group = w_project.shape[2]
-    steps = 8
+    steps = depth // 16
     parts = col_size // 2
     stride = depth + 8
     any_spec = pl.BlockSpec(memory_space=pl.ANY)
     vmem_spec = pl.BlockSpec(memory_space=pltpu.VMEM)
     bf16, f32 = jnp.bfloat16, jnp.float32
-    single_out, left, right = pl.pallas_call(
+    single_out, left, right, part = pl.pallas_call(
         functools.partial(attend_kernel, row_size, col_size, heads, tile_cols, stride),
         out_shape=(
             jax.ShapeDtypeStruct((halves, col_size, rows_each, width), bf16),
             jax.ShapeDtypeStruct((tile_rows, wide), f32),
             jax.ShapeDtypeStruct((tile_cols, wide), f32),
+            jax.ShapeDtypeStruct((depth, tile_cols, wide), bf16),
         ),
-        in_specs=[any_spec] * 7,
-        out_specs=[any_spec, vmem_spec, vmem_spec],
+        in_specs=[any_spec] * 10,
+        out_specs=[any_spec, vmem_spec, vmem_spec, any_spec],
         scratch_shapes=[
             pltpu.VMEM((tile_rows, width), bf16),
             pltpu.VMEM((halves, depth, tile_cols, wide), bf16),
@@ -790,9 +930,14 @@
             pltpu.VMEM((col_size, rows_each, LANES), f32),
             pltpu.VMEM((col_size, rows_each, LANES), f32),
             pltpu.VMEM((halves, rows_each, width), bf16),
-            pltpu.VMEM((2, halves * wide, halves * wide), bf16),
+            pltpu.VMEM((halves * wide, halves * wide), bf16),
             pltpu.VMEM((halves, 2 * LANES, width), bf16),
-            pltpu.SemaphoreType.DMA((9 + halves,)),
+            pltpu.VMEM(w_pairout.shape, bf16),
+            pltpu.VMEM((2 * wide, 2 * wide), bf16),
+            pltpu.VMEM(w_up.shape, bf16),
+            pltpu.VMEM(w_down.shape, bf16),
+            pltpu.VMEM((depth, tile_cols, wide), bf16),
+            pltpu.SemaphoreType.DMA((12 + halves,)),
             pltpu.SemaphoreType.DMA((steps,)),
             pltpu.SemaphoreType.DMA((6, col_size - 1)),
             pltpu.SemaphoreType.DMA((6, col_size - 1)),
@@ -810,14 +955,17 @@
         name="attend",
     )(
         single,
-        pair.reshape(halves, depth, tile_cols, wide),
+        pair,
         mask.reshape(mask.shape[0] // LANES, LANES),
         w_bias.T,
         w_project,
         w_out,
         w_factors,
-    )
-    return single_out.reshape(tile_rows, width), left, right
+        w_pairout,
+        w_up,
+        w_down,
+    )
+    return single_out.reshape(tile_rows, width), left, right, part
 
 
 def fits(row_size, col_size, single, pair, mask, w_bias, w_project, w_factors):
@@ -834,6 +982,7 @@
         and tile_cols % (8 * col_size) == 0
         and col_size == 2 * row_size
         and row_size % 2 == 0
+        and tile_cols % (2 * update_block) == 0
         and mask.shape[0] % LANES == 0
     )
 
@@ -842,10 +991,14 @@
     row_size, col_size,
     single, pair, residue_mask, w_bias, w_project, w_out, w_factors, w_pairout, w_up, w_down
 ):
-    single_out, left, right = attend(
-        single, pair, residue_mask, w_bias, w_project, w_out, w_factors, row_size, col_size
-    )
-    return (single_out, update_pair(pair, left, right, w_pairout, w_up, w_down))
+    shape = pair.shape
+    pair = pair.reshape(2, shape[0] // 2, *shape[1:])
+    single_out, left, right, part = attend(
+        single, pair, residue_mask, w_bias, w_project, w_out, w_factors, w_pairout, w_up, w_down,
+        row_size, col_size,
+    )
+    single_out, pair = finish(single_out, pair, part, left, right, w_pairout, w_up, w_down)
+    return single_out, pair.reshape(shape)
 
 
 def dispatch(row_size, col_size, *arrays):

time: 55.3 us -> 52.8 us (0.955)
  Pallas kernels: 53.8 us -> 52 us
  local copies, waits for them, and re-layouts: 0.71 us -> 0 us
    pallas_call x1, Pallas kernels: 11.1 us -> 6.23 us  [finish(): pl.pallas_call(finish_kernel, out_shape=(jax.ShapeDtypeStruct(single.shap...]
    pallas_call x1, Pallas kernels: 42.6 us -> 45.7 us  [attend(): pl.pallas_call(functools.partial(attend_kernel, row_size, col_size, heads...]
    unnamed x3 -> x0, local copies, waits for them, and re-layouts: 0.71 us -> none
where the time goes in v3:
time: 52.8 us; the launch traced here: 52.6 us
  Pallas kernels  52 us (98%)
  between operations  0.64 us (1%)
    pallas_call x1, Pallas kernels, attend(): pl.pallas_call(functools.partial(attend_kernel, row_size, col_size, heads...  45.7 us
    pallas_call x1, Pallas kernels, finish(): pl.pallas_call(finish_kernel, out_shape=(jax.ShapeDtypeStruct(single.shap...  6.23 us

profile of v3, /device:TPU:0, one launch (start us, length us, event | category | flops | bytes accessed | tf_op | source)
XLA Modules:
  0.0 52.6 jit_solution(1087534747047742667)
XLA Ops:
  0.6 45.7 %attend.1 = (bf16[2,8,8,1024]{3,2,1,0:T(8,128)(2,1)}, f32[128,128]{1,0:T(8,128)}, f32[64,128]{1,0:T(8,128)}, bf16[64,64,128]{2,1,0:T(8,128)(2,1)}) custom-call(bf16[128,1024]{1,0:T(8,128)(2,1)} %single.1, bf16[2,64,64,128]{3,2,1,0:T(8,128)(2,1)} %bitcast.5, s32[4,128]{1,0:T(4,128)} %bitcast.9, bf16[32,128]{1,0:T(8,128)(2,1)} %bitcast.8, ...), custom_call_target="tpu_custom_call" | custom-call | tf_op jit(solution)/shard_map/attend/pallas_call | solution.py:899
  46.4 6.2 %finish.1 = (bf16[128,1024]{1,0:T(8,128)(2,1)}, bf16[2,64,64,128]{3,2,1,0:T(8,128)(2,1)}) custom-call(bf16[128,1024]{1,0:T(8,128)(2,1)} %bitcast.7, bf16[2,64,64,128]{3,2,1,0:T(8,128)(2,1)} %bitcast.6, bf16[64,64,128]{2,1,0:T(8,128)(2,1)} %get-tuple-element.9.part, f32[128,128]{1,0:T(8,128)} %get-tuple-element.10.left, f32[64,128]{1,0:T(8,128)} %get-tuple-element.11.right, ...), custom_call_target="tpu_custom_call" | custom-call | tf_op jit(solution)/shard_map/finish/pallas_call | solution.py:862

commit v4 on v3

--- a/solution.py
+++ b/solution.py
@@ -354,7 +354,7 @@
     st_send, st_recv, left_send, right_send, left_recv, right_recv, so_send, centre_v, spread_v,
     pairout_v, twice_v, up_v, down_v, part_v,
     load_sems, pair_sems, col_send, col_recv, fan_send, fan_recv,
-    kv_sent, kv_came, kv_relayed, q_sent, q_came, o_sent, o_came,
+    plane_sent, plane_came, kv_sent, kv_came, kv_relayed, q_sent, q_came, o_sent, o_came,
 ):
     me_row = lax.axis_index("rows")
     me_col = lax.axis_index("cols")
@@ -380,7 +380,7 @@
         pltpu.make_async_copy(source, target, load_sems.at[index])
         for index, (source, target) in enumerate(
             [(single, single_v)]
-            + [(w_project.at[part], project_v.at[part]) for part in (1, 2, 0, 3)]
+            + [(w_project.at[part], project_v.at[part]) for part in range(4)]
             + [(w_bias, bias_w), (mask, mask_v)]
             + [
                 (single.at[pl.ds(half * depth + me_col * rows_each, rows_each)], own_single.at[half])
@@ -448,6 +448,7 @@
                 pl.when(condition)(functools.partial(act, copy))
 
     kind_mine = lax.rem(me_row, 2)
+    me_plane = me_row // 2
     row_mate = me_row + 1 - 2 * kind_mine
     col_mate = me_col + 1 - 2 * lax.rem(me_col, 2)
 
@@ -492,27 +493,52 @@
 
     loads[0].wait()
     normed = layer_norm(single_v[...]).astype(jnp.bfloat16)
+    def project(*kinds):
+        weights = [project_v[kind] for kind in kinds]
+        return jnp.dot(
+            normed, jnp.concatenate(weights, axis=1), preferred_element_type=jnp.float32
+        )
+
     loads[1].wait()
+    q_recv[me_col] = project(0).astype(jnp.bfloat16)
+    pl.semaphore_wait(barrier, total - 1)
+    peers = [lax.rem(me_col + 2 * step, col_size) for step in range(1, col_size // 2)]
+    q_copies = [send_query(me_col, to, slot) for slot, to in enumerate(peers)]
+    q_copies.append(send_query(me_col, col_mate, len(peers)))
+    for copy in q_copies:
+        copy.start()
     loads[2].wait()
-    key_value = jnp.dot(
-        normed,
-        jnp.concatenate([project_v[1], project_v[2]], axis=1),
-        preferred_element_type=jnp.float32,
-    ).astype(jnp.bfloat16)
+    loads[3].wait()
+    key_value = project(1, 2).astype(jnp.bfloat16)
     for half in range(halves):
         for kind in range(2):
-            kv_send[half, kind] = key_value[
+            kv_send[me_plane, half, kind] = key_value[
                 half * tile_cols : (half + 1) * tile_cols, kind * group : (kind + 1) * group
             ]
-    pl.semaphore_wait(barrier, total - 1)
+    planes = row_size // 2
+    plane_copies = []
+    for step in range(1, planes):
+        plane = lax.rem(me_plane + step, planes)
+        copy = pltpu.make_async_remote_copy(
+            src_ref=kv_send.at[me_plane],
+            dst_ref=kv_send.at[me_plane],
+            send_sem=plane_sent.at[step - 1],
+            recv_sem=plane_came.at[step - 1],
+            device_id={"rows": 2 * plane + kind_mine},
+            device_id_type=pl.DeviceIdType.MESH,
+        )
+        copy.start()
+        plane_copies.append(copy)
     kv_copies = []
-    for step in range(row_size // 2):
-        for kind in range(2):
-            for half in range(halves):
-                to = halves * me_row + half
-                row = 2 * lax.rem(me_row // 2 + step, row_size // 2) + kind
+
+    def send_keys(step):
+        plane = lax.rem(me_plane + planes - step, planes)
+        for half in range(halves):
+            for kind in range(2):
+                to = halves * (2 * plane + kind_mine) + half
+                row = 2 * me_plane + kind
                 copy = pltpu.make_async_remote_copy(
-                    src_ref=kv_send.at[half, kind],
+                    src_ref=kv_send.at[plane, half, kind],
                     dst_ref=kv_recv.at[me_col, kind],
                     send_sem=kv_sent.at[(step * 2 + kind) * halves + half],
                     recv_sem=kv_came.at[kind, me_col],
@@ -520,29 +546,12 @@
                     device_id_type=pl.DeviceIdType.MESH,
                 )
                 here = jnp.logical_and(row == me_row, to == me_col)
-                copies_of = (copy, None if step else jnp.logical_not(here))
-                kv_copies.append(copies_of)
-    on_some(kv_copies, lambda copy: copy.start())
-
-    @pl.when(mine)
-    def _():
-        kv_recv[me_col, kind_mine] = kv_send[half_mine, kind_mine]
-
-    loads[3].wait()
+                kv_copies.append((copy, jnp.logical_not(here)))
+        on_some(kv_copies[-2 * halves :], lambda copy: copy.start())
+
+    send_keys(0)
     loads[4].wait()
-    query_gate = jnp.dot(
-        normed,
-        jnp.concatenate([project_v[0], project_v[3]], axis=1),
-        preferred_element_type=jnp.float32,
-    )
-    q_recv[me_col] = query_gate[:, :group].astype(jnp.bfloat16)
-    peers = [lax.rem(me_col + 2 * step, col_size) for step in range(1, col_size // 2)]
-    mates = [lax.rem(col_mate + 2 * step, col_size) for step in range(1, col_size // 2)]
-    q_copies = [send_query(me_col, to, slot) for slot, to in enumerate(peers)]
-    q_copies.append(send_query(me_col, col_mate, len(peers)))
-    for copy in q_copies:
-        copy.start()
-    gate_send[...] = jax.nn.sigmoid(query_gate[:, group:]).reshape(halves, depth, group)
+    gate_send[...] = jax.nn.sigmoid(project(3)).reshape(halves, depth, group)
 
     def own_rows(to):
         return pl.ds(pl.multiple_of(to * rows_each, rows_each), rows_each)
@@ -578,23 +587,14 @@
         spread_v[half, :LANES] = picked.astype(jnp.bfloat16)
         spread_v[half, LANES:] = picked.astype(jnp.bfloat16)
 
-    relays = []
-    for part in range(col_size):
-        copy = relay_keys(part, kind_mine, part)
-        pl.when(jnp.logical_not(jnp.logical_and(mine, part == me_col)))(copy.wait_recv)
-        copy.start()
-        relays.append(copy)
-    for slot, peer in enumerate(peers):
-        copy = send_query(peer, col_mate, col_size // 2 + slot)
-        copy.wait_recv()
-        copy.start()
-        relays.append(copy)
-    for part in range(col_size):
-        relay_keys(part, 1 - kind_mine, part).wait_recv()
-    for part in [col_mate] + mates:
-        send_query(part, col_mate, 0).wait_recv()
-    gate_copies = to_cols(1, lambda to: gate_send.at[:, own_rows(to)], gate_recv.at[me_col])
-    gate_recv[me_col] = gate_send[:, own_rows(me_col)]
+    for step in range(1, planes):
+        plane_copies[step - 1].wait_recv()
+        send_keys(step)
+    own_key = lax.rem(owner, 2) == kind_mine
+
+    @pl.when(own_key)
+    def _():
+        kv_recv[me_col, kind_mine] = kv_send[owner // 2, half_mine, kind_mine]
 
     length = jnp.sum(jnp.sum(mask_v[...], axis=1, keepdims=True), axis=0, keepdims=True)
     lane = lane_iota((depth, LANES))
@@ -662,6 +662,7 @@
 
     parts, _, _, part_width = o_send.shape
     each = part_width // group
+    col_side = lax.rem(me_col, each)
 
     def o_copy(step, shift):
         to = lax.rem(me_col + shift, col_size)
@@ -674,7 +675,29 @@
             device_id_type=pl.DeviceIdType.MESH,
         )
 
-    def attend_step(step, _):
+    def relay_query(part):
+        return send_query(part, col_mate, col_size // 2 + part // each)
+
+    def attend_step(turn, _):
+        step = lax.rem(me_col // each + turn, parts)
+        near = step * each + col_side
+        far = step * each + 1 - col_side
+
+        @pl.when(turn > 0)
+        def _():
+            relay_query(near).wait_recv()
+            relay_query(near).start()
+
+        for index in range(each):
+            part = step * each + index
+            copy = relay_keys(part, kind_mine, part)
+            own = jnp.logical_and(own_key, part == me_col)
+            pl.when(jnp.logical_not(own))(copy.wait_recv)
+            copy.start()
+        relay_query(far).wait_recv()
+        for index in range(each):
+            part = step * each + index
+            relay_keys(part, 1 - kind_mine, part).wait_recv()
         for index in range(each):
             o_send[step, :, :, index * group : (index + 1) * group] = attend_part(
                 step * each + index
@@ -684,6 +707,10 @@
         return 0
 
     lax.fori_loop(0, parts, attend_step, 0)
+    relays = [relay_keys(part, kind_mine, part) for part in range(col_size)]
+    relays += [relay_query(peer) for peer in peers]
+    gate_copies = to_cols(1, lambda to: gate_send.at[:, own_rows(to)], gate_recv.at[me_col])
+    gate_recv[me_col] = gate_send[:, own_rows(me_col)]
 
     st_copies = to_cols(2, lambda to: st_send.at[own_rows(to)], st_recv.at[me_col])
     st_recv[me_col] = st_send[own_rows(me_col)]
@@ -762,7 +789,7 @@
 
     twice_v[...] = twice(pairout_v[...])
     block = update_block
-    starts = depth // (2 * block)
+    starts = part_v.shape[0] // (2 * block)
 
     def part_copy(step):
         rows = pl.ds(step * 2 * block, 2 * block)
@@ -770,8 +797,9 @@
 
     def update_step(step, _):
         first = step * 2 * block
+        half = first // depth
         part_v[pl.ds(first, 2 * block)] = update_rows(
-            lambda index: pair_v[0, pl.ds(first + index * block, block)],
+            lambda index: pair_v[half, pl.ds(first - half * depth + index * block, block)],
             lambda index: left_out[pl.ds(pl.multiple_of(first + index * block, 8), block)],
             right_out[...],
             block,
@@ -785,7 +813,7 @@
 
     lax.fori_loop(0, starts, update_step, 0)
 
-    for copies in (q_copies, relays, gate_copies, st_copies, o_copies, left_copies, so_copies):
+    for copies in (q_copies, relays, plane_copies, gate_copies, st_copies, o_copies, left_copies, so_copies):
         for copy in copies:
             copy.wait_send()
     on_some(kv_copies, lambda copy: copy.wait_send())
@@ -800,82 +828,84 @@
 def finish_kernel(
     single, pair, part, left, right, w_pairout, w_up, w_down,
     single_out, pair_out,
-    single_v, pair_v, part_v, done_v, centre_v, twice_v, sems, out_sems,
+    single_v, pair_v, part_v, done_v, left_v, right_v, pairout_v, up_v, down_v,
+    centre_v, twice_v, sems, out_sems,
 ):
-    _, depth, tile_cols, wide = pair.shape
-    block = update_block
-    steps = depth // (2 * block)
-
-    def rows(step):
-        return pl.ds(step * 2 * block, 2 * block)
-
+    tile_rows, tile_cols, wide = pair.shape
+    done = part.shape[0]
+    block = (tile_rows - done) // 2
+    rows = pl.ds(done, 2 * block)
     loads = [
-        pltpu.make_async_copy(pair.at[1, rows(step)], pair_v.at[rows(step)], sems.at[2 + step])
-        for step in range(steps)
-    ]
-    through = [
-        (pltpu.make_async_copy(part, part_v, sems.at[0]),
-         pltpu.make_async_copy(part_v, pair_out.at[0], out_sems.at[0])),
-        (pltpu.make_async_copy(single, single_v, sems.at[1]),
-         pltpu.make_async_copy(single_v, single_out, out_sems.at[1])),
+        pltpu.make_async_copy(source, target, sems.at[index])
+        for index, (source, target) in enumerate(
+            [
+                (w_pairout, pairout_v),
+                (pair.at[rows], pair_v),
+                (left.at[rows], left_v),
+                (right, right_v),
+                (w_up, up_v),
+                (w_down, down_v),
+                (part, part_v),
+                (single, single_v),
+            ]
+        )
     ]
     for copy in loads:
         copy.start()
-    for copy, _ in through:
-        copy.start()
+    stores = [
+        pltpu.make_async_copy(part_v, pair_out.at[pl.ds(0, done)], out_sems.at[0]),
+        pltpu.make_async_copy(single_v, single_out, out_sems.at[1]),
+        pltpu.make_async_copy(done_v, pair_out.at[rows], out_sems.at[2]),
+    ]
     centre_v[...] = centre_matrix(wide, 2)
-    twice_v[...] = twice(w_pairout[...])
-    stores = []
-    for step in range(steps):
-        loads[step].wait()
-        first = step * 2 * block
-        done_v[rows(step)] = update_rows(
-            lambda index: pair_v[first + index * block : first + (index + 1) * block],
-            lambda index: left[depth + first + index * block : depth + first + (index + 1) * block],
-            right[...],
-            block,
-            centre_v[...],
-            twice_v[...],
-            w_up[...],
-            w_down[...],
-        )
-        store = pltpu.make_async_copy(
-            done_v.at[rows(step)], pair_out.at[1, rows(step)], out_sems.at[2 + step]
-        )
+    for copy in loads[:6]:
+        copy.wait()
+    twice_v[...] = twice(pairout_v[...])
+    for copy, store in zip(loads[6:], stores):
+        copy.wait()
         store.start()
-        stores.append(store)
-        if step == 0:
-            for load, later in through:
-                load.wait()
-                later.start()
-                stores.append(later)
+    done_v[...] = update_rows(
+        lambda index: pair_v[index * block : (index + 1) * block],
+        lambda index: left_v[index * block : (index + 1) * block],
+        right_v[...],
+        block,
+        centre_v[...],
+        twice_v[...],
+        up_v[...],
+        down_v[...],
+    )
+    stores[2].start()
     for store in stores:
         store.wait()
 
 
 def finish(single, pair, part, left, right, w_pairout, w_up, w_down):
-    halves, depth, tile_cols, wide = pair.shape
-    steps = depth // (2 * update_block)
+    tile_rows, tile_cols, wide = pair.shape
+    done = part.shape[0]
     any_spec = pl.BlockSpec(memory_space=pl.ANY)
-    vmem_spec = pl.BlockSpec(memory_space=pltpu.VMEM)
-    bf16 = jnp.bfloat16
+    bf16, f32 = jnp.bfloat16, jnp.float32
     return pl.pallas_call(
         finish_kernel,
         out_shape=(
             jax.ShapeDtypeStruct(single.shape, bf16),
             jax.ShapeDtypeStruct(pair.shape, bf16),
         ),
-        in_specs=[any_spec] * 3 + [vmem_spec] * 5,
+        in_specs=[any_spec] * 8,
         out_specs=[any_spec] * 2,
         scratch_shapes=[
             pltpu.VMEM(single.shape, bf16),
-            pltpu.VMEM((depth, tile_cols, wide), bf16),
-            pltpu.VMEM((depth, tile_cols, wide), bf16),
-            pltpu.VMEM((depth, tile_cols, wide), bf16),
+            pltpu.VMEM((tile_rows - done, tile_cols, wide), bf16),
+            pltpu.VMEM(part.shape, bf16),
+            pltpu.VMEM((tile_rows - done, tile_cols, wide), bf16),
+            pltpu.VMEM((tile_rows - done, wide), f32),
+            pltpu.VMEM(right.shape, f32),
+            pltpu.VMEM(w_pairout.shape, bf16),
+            pltpu.VMEM(w_up.shape, bf16),
+            pltpu.VMEM(w_down.shape, bf16),
             pltpu.VMEM((2 * wide, 2 * wide), bf16),
             pltpu.VMEM((2 * wide, 2 * wide), bf16),
-            pltpu.SemaphoreType.DMA((2 + steps,)),
-            pltpu.SemaphoreType.DMA((2 + steps,)),
+            pltpu.SemaphoreType.DMA((8,)),
+            pltpu.SemaphoreType.DMA((3,)),
         ],
         name="finish",
     )(single, pair, part, left, right, w_pairout, w_up, w_down)
@@ -892,6 +922,7 @@
     group = w_project.shape[2]
     steps = depth // 16
     parts = col_size // 2
+    part_rows = tile_rows - 2 * update_block
     stride = depth + 8
     any_spec = pl.BlockSpec(memory_space=pl.ANY)
     vmem_spec = pl.BlockSpec(memory_space=pltpu.VMEM)
@@ -902,7 +933,7 @@
             jax.ShapeDtypeStruct((halves, col_size, rows_each, width), bf16),
             jax.ShapeDtypeStruct((tile_rows, wide), f32),
             jax.ShapeDtypeStruct((tile_cols, wide), f32),
-            jax.ShapeDtypeStruct((depth, tile_cols, wide), bf16),
+            jax.ShapeDtypeStruct((part_rows, tile_cols, wide), bf16),
         ),
         in_specs=[any_spec] * 10,
         out_specs=[any_spec, vmem_spec, vmem_spec, any_spec],
@@ -915,7 +946,7 @@
             pltpu.VMEM(w_out.shape, bf16),
             pltpu.VMEM(w_factors.shape, bf16),
             pltpu.VMEM((halves, rows_each, width), bf16),
-            pltpu.VMEM((halves, 2, tile_cols, group), bf16),
+            pltpu.VMEM((row_size // 2, halves, 2, tile_cols, group), bf16),
             pltpu.VMEM((col_size, 2, tile_cols, group), bf16),
             pltpu.VMEM((col_size, tile_rows, group), bf16),
             pltpu.VMEM((halves, depth, group), f32),
@@ -936,17 +967,19 @@
             pltpu.VMEM((2 * wide, 2 * wide), bf16),
             pltpu.VMEM(w_up.shape, bf16),
             pltpu.VMEM(w_down.shape, bf16),
-            pltpu.VMEM((depth, tile_cols, wide), bf16),
+            pltpu.VMEM((part_rows, tile_cols, wide), bf16),
             pltpu.SemaphoreType.DMA((12 + halves,)),
             pltpu.SemaphoreType.DMA((steps,)),
             pltpu.SemaphoreType.DMA((6, col_size - 1)),
             pltpu.SemaphoreType.DMA((6, col_size - 1)),
             pltpu.SemaphoreType.DMA((2, row_size * halves)),
             pltpu.SemaphoreType.DMA((2, col_size)),
+            pltpu.SemaphoreType.DMA((row_size // 2 - 1,)),
+            pltpu.SemaphoreType.DMA((row_size // 2 - 1,)),
             pltpu.SemaphoreType.DMA((row_size * halves,)),
             pltpu.SemaphoreType.DMA((2, col_size)),
             pltpu.SemaphoreType.DMA((col_size,)),
-            pltpu.SemaphoreType.DMA((col_size,)),
+            pltpu.SemaphoreType.DMA((2 * col_size,)),
             pltpu.SemaphoreType.DMA((col_size,)),
             pltpu.SemaphoreType.DMA((parts, col_size - 1)),
             pltpu.SemaphoreType.DMA((parts, col_size - 1)),
@@ -992,13 +1025,11 @@
     single, pair, residue_mask, w_bias, w_project, w_out, w_factors, w_pairout, w_up, w_down
 ):
     shape = pair.shape
-    pair = pair.reshape(2, shape[0] // 2, *shape[1:])
     single_out, left, right, part = attend(
-        single, pair, residue_mask, w_bias, w_project, w_out, w_factors, w_pairout, w_up, w_down,
-        row_size, col_size,
-    )
-    single_out, pair = finish(single_out, pair, part, left, right, w_pairout, w_up, w_down)
-    return single_out, pair.reshape(shape)
+        single, pair.reshape(2, shape[0] // 2, *shape[1:]), residue_mask,
+        w_bias, w_project, w_out, w_factors, w_pairout, w_up, w_down, row_size, col_size,
+    )
+    return tuple(finish(single_out, pair, part, left, right, w_pairout, w_up, w_down))
 
 
 def dispatch(row_size, col_size, *arrays):

time: 52.8 us -> 50.7 us (0.960)
  Pallas kernels: 52 us -> 49.9 us
    pallas_call x1, Pallas kernels: 6.23 us -> 4.25 us  [finish(): pl.pallas_call(finish_kernel, out_shape=(jax.ShapeDtypeStruct(single.shap...]
where the time goes in v4:
time: 50.7 us; the launch traced here: 50.5 us
  Pallas kernels  49.9 us (98%)
  between operations  0.64 us (1%)
    pallas_call x1, Pallas kernels, attend(): pl.pallas_call(functools.partial(attend_kernel, row_size, col_size, heads...  45.7 us
    pallas_call x1, Pallas kernels, finish(): pl.pallas_call(finish_kernel, out_shape=(jax.ShapeDtypeStruct(single.shap...  4.25 us

profile of v4, /device:TPU:0, one launch (start us, length us, event | category | flops | bytes accessed | tf_op | source)
XLA Modules:
  0.0 50.5 jit_solution(6960858897889760159)
XLA Ops:
  0.6 45.7 %attend.1 = (bf16[2,8,8,1024]{3,2,1,0:T(8,128)(2,1)}, f32[128,128]{1,0:T(8,128)}, f32[64,128]{1,0:T(8,128)}, bf16[96,64,128]{2,1,0:T(8,128)(2,1)}) custom-call(bf16[128,1024]{1,0:T(8,128)(2,1)} %single.1, bf16[2,64,64,128]{3,2,1,0:T(8,128)(2,1)} %bitcast.4, s32[4,128]{1,0:T(4,128)} %bitcast.7, bf16[32,128]{1,0:T(8,128)(2,1)} %bitcast.6, ...), custom_call_target="tpu_custom_call" | custom-call | tf_op jit(solution)/shard_map/attend/pallas_call | solution.py:930
  46.3 4.2 %finish.1 = (bf16[128,1024]{1,0:T(8,128)(2,1)}, bf16[128,64,128]{2,1,0:T(8,128)(2,1)}) custom-call(bf16[128,1024]{1,0:T(8,128)(2,1)} %bitcast.5, bf16[128,64,128]{2,1,0:T(8,128)(2,1)} %pair.1, bf16[96,64,128]{2,1,0:T(8,128)(2,1)} %get-tuple-element.7.part, f32[128,128]{1,0:T(8,128)} %get-tuple-element.8.left, f32[64,128]{1,0:T(8,128)} %get-tuple-element.9.right, ...), custom_call_target="tpu_custom_call" | custom-call | tf_op jit(solution)/shard_map/finish/pallas_call | solution.py:887

commit v5 on v4

--- a/solution.py
+++ b/solution.py
@@ -359,16 +359,6 @@
     me_row = lax.axis_index("rows")
     me_col = lax.axis_index("cols")
     total = row_size * col_size
-    barrier = pltpu.get_barrier_semaphore()
-    me = me_row * col_size + me_col
-    for step in range(1, total):
-        to = lax.rem(me + step, total)
-        pl.semaphore_signal(
-            barrier,
-            inc=1,
-            device_id={"rows": to // col_size, "cols": lax.rem(to, col_size)},
-            device_id_type=pl.DeviceIdType.MESH,
-        )
     halves, depth, _, wide = pair.shape
     tile_rows, width = single.shape
     group = w_project.shape[2]
@@ -392,6 +382,16 @@
     ]
     for copy in loads[:7]:
         copy.start()
+    barrier = pltpu.get_barrier_semaphore()
+    me = me_row * col_size + me_col
+    for step in range(1, total):
+        to = lax.rem(me + step, total)
+        pl.semaphore_signal(
+            barrier,
+            inc=1,
+            device_id={"rows": to // col_size, "cols": lax.rem(to, col_size)},
+            device_id_type=pl.DeviceIdType.MESH,
+        )
 
     def pair_load(step):
         part = pl.ds(step * chunk, chunk)
@@ -559,6 +559,13 @@
     loads[5].wait()
     loads[6].wait()
 
+    parts, _, _, part_width = o_send.shape
+    each = part_width // group
+    col_side = lax.rem(me_col, each)
+
+    def relay_query(part):
+        return send_query(part, col_mate, col_size // 2 + part // each)
+
     def bias_step(step, _):
         pair_load(step).wait()
         parts = [
@@ -578,7 +585,32 @@
             ]
         return 0
 
-    lax.fori_loop(0, depth // chunk, bias_step, 0)
+    bias_steps = depth // chunk
+    lax.fori_loop(0, bias_steps // 2, bias_step, 0)
+    for step in range(1, planes):
+        plane_copies[step - 1].wait_recv()
+        send_keys(step)
+    own_key = lax.rem(owner, 2) == kind_mine
+
+    @pl.when(own_key)
+    def _():
+        kv_recv[me_col, kind_mine] = kv_send[owner // 2, half_mine, kind_mine]
+
+    lax.fori_loop(bias_steps // 2, bias_steps, bias_step, 0)
+    relays = [relay_query(peer) for peer in peers]
+    for copy in relays:
+        copy.wait_recv()
+        copy.start()
+    for turn in range(parts):
+        for index in range(each):
+            part = lax.rem(me_col // each + turn, parts) * each + index
+            copy = relay_keys(part, kind_mine, part)
+            own = jnp.logical_and(own_key, part == me_col)
+            pl.when(jnp.logical_not(own))(copy.wait_recv)
+            copy.start()
+            relays.append(copy)
+    gate_copies = to_cols(1, lambda to: gate_send.at[:, own_rows(to)], gate_recv.at[me_col])
+    gate_recv[me_col] = gate_send[:, own_rows(me_col)]
 
     lane_row = lane_iota((2 * halves * heads, width))
     place = lax.broadcasted_iota(jnp.int32, (2 * halves * heads, width), 0)
@@ -586,15 +618,6 @@
         picked = jnp.where(place == half * heads + lane_row // head_width, 1.0, 0.0)
         spread_v[half, :LANES] = picked.astype(jnp.bfloat16)
         spread_v[half, LANES:] = picked.astype(jnp.bfloat16)
-
-    for step in range(1, planes):
-        plane_copies[step - 1].wait_recv()
-        send_keys(step)
-    own_key = lax.rem(owner, 2) == kind_mine
-
-    @pl.when(own_key)
-    def _():
-        kv_recv[me_col, kind_mine] = kv_send[owner // 2, half_mine, kind_mine]
 
     length = jnp.sum(jnp.sum(mask_v[...], axis=1, keepdims=True), axis=0, keepdims=True)
     lane = lane_iota((depth, LANES))
@@ -660,10 +683,6 @@
         ]
         return jnp.concatenate(pieces, axis=1).astype(jnp.bfloat16)
 
-    parts, _, _, part_width = o_send.shape
-    each = part_width // group
-    col_side = lax.rem(me_col, each)
-
     def o_copy(step, shift):
         to = lax.rem(me_col + shift, col_size)
         return pltpu.make_async_remote_copy(
@@ -675,25 +694,9 @@
             device_id_type=pl.DeviceIdType.MESH,
         )
 
-    def relay_query(part):
-        return send_query(part, col_mate, col_size // 2 + part // each)
-
     def attend_step(turn, _):
         step = lax.rem(me_col // each + turn, parts)
-        near = step * each + col_side
         far = step * each + 1 - col_side
-
-        @pl.when(turn > 0)
-        def _():
-            relay_query(near).wait_recv()
-            relay_query(near).start()
-
-        for index in range(each):
-            part = step * each + index
-            copy = relay_keys(part, kind_mine, part)
-            own = jnp.logical_and(own_key, part == me_col)
-            pl.when(jnp.logical_not(own))(copy.wait_recv)
-            copy.start()
         relay_query(far).wait_recv()
         for index in range(each):
             part = step * each + index
@@ -707,11 +710,6 @@
         return 0
 
     lax.fori_loop(0, parts, attend_step, 0)
-    relays = [relay_keys(part, kind_mine, part) for part in range(col_size)]
-    relays += [relay_query(peer) for peer in peers]
-    gate_copies = to_cols(1, lambda to: gate_send.at[:, own_rows(to)], gate_recv.at[me_col])
-    gate_recv[me_col] = gate_send[:, own_rows(me_col)]
-
     st_copies = to_cols(2, lambda to: st_send.at[own_rows(to)], st_recv.at[me_col])
     st_recv[me_col] = st_send[own_rows(me_col)]
     for step in range(parts):
@@ -766,18 +764,18 @@
     right_copies = fan_copies(1, lambda half: right_send, right_recv)
     on_fan(right_copies, lambda copy: copy.start())
     left_copies = to_cols(4, lambda to: left_send, left_recv.at[me_col])
+    left_recv[me_col] = left
+
+    @pl.when(mine)
+    def _():
+        right_recv[me_col] = right_send[...]
+
+    fan_wait(1, lambda half: right_send, right_recv)
+    for copy in left_copies:
+        copy.wait_recv()
     so_copies = to_cols(5, lambda to: so_send, single_out.at[:, me_col])
     own_copy = pltpu.make_async_copy(so_send, single_out.at[:, me_col], load_sems.at[0])
     own_copy.start()
-    left_recv[me_col] = left
-
-    @pl.when(mine)
-    def _():
-        right_recv[me_col] = right_send[...]
-
-    fan_wait(1, lambda half: right_send, right_recv)
-    for copy in left_copies:
-        copy.wait_recv()
     left = left_recv[...].reshape(depth, LANES)
     turned = pltpu.roll(left, shift, axis=1)
     low = lane_iota(left.shape) < shift

time: 50.7 us -> 44.5 us (0.88)
  Pallas kernels: 49.9 us -> 43.7 us
    pallas_call x1, Pallas kernels: 45.7 us -> 39.4 us  [attend(): pl.pallas_call(functools.partial(attend_kernel, row_size, col_size, heads...]
where the time goes in v5:
time: 44.5 us; the launch traced here: 44.3 us
  Pallas kernels  43.7 us (98%)
  between operations  0.64 us (1%)
    pallas_call x1, Pallas kernels, attend(): pl.pallas_call(functools.partial(attend_kernel, row_size, col_size, heads...  39.4 us
    pallas_call x1, Pallas kernels, finish(): pl.pallas_call(finish_kernel, out_shape=(jax.ShapeDtypeStruct(single.shap...  4.25 us

profile of v5, /device:TPU:0, one launch (start us, length us, event | category | flops | bytes accessed | tf_op | source)
XLA Modules:
  0.0 44.3 jit_solution(15967280261918144810)
XLA Ops:
  0.6 39.4 %attend.1 = (bf16[2,8,8,1024]{3,2,1,0:T(8,128)(2,1)}, f32[128,128]{1,0:T(8,128)}, f32[64,128]{1,0:T(8,128)}, bf16[96,64,128]{2,1,0:T(8,128)(2,1)}) custom-call(bf16[128,1024]{1,0:T(8,128)(2,1)} %single.1, bf16[2,64,64,128]{3,2,1,0:T(8,128)(2,1)} %bitcast.4, s32[4,128]{1,0:T(4,128)} %bitcast.7, bf16[32,128]{1,0:T(8,128)(2,1)} %bitcast.6, ...), custom_call_target="tpu_custom_call" | custom-call | tf_op jit(solution)/shard_map/attend/pallas_call | solution.py:928
  40.1 4.2 %finish.1 = (bf16[128,1024]{1,0:T(8,128)(2,1)}, bf16[128,64,128]{2,1,0:T(8,128)(2,1)}) custom-call(bf16[128,1024]{1,0:T(8,128)(2,1)} %bitcast.5, bf16[128,64,128]{2,1,0:T(8,128)(2,1)} %pair.1, bf16[96,64,128]{2,1,0:T(8,128)(2,1)} %get-tuple-element.7.part, f32[128,128]{1,0:T(8,128)} %get-tuple-element.8.left, f32[64,128]{1,0:T(8,128)} %get-tuple-element.9.right, ...), custom_call_target="tpu_custom_call" | custom-call | tf_op jit(solution)/shard_map/finish/pallas_call | solution.py:885

commit v6 on v5

--- a/solution.py
+++ b/solution.py
@@ -348,11 +348,11 @@
 def attend_kernel(
     row_size, col_size, heads, tile_cols, stride,
     single, pair, mask, w_bias, w_project, w_out, w_factors, w_pairout, w_up, w_down,
-    single_out, left_out, right_out, part_out,
+    single_out, pair_out,
     single_v, pair_v, mask_v, bias_w, project_v, out_v, factors_v, own_single,
     kv_send, kv_recv, q_recv, gate_send, gate_recv, bias_v, o_send, o_recv,
-    st_send, st_recv, left_send, right_send, left_recv, right_recv, so_send, centre_v, spread_v,
-    pairout_v, twice_v, up_v, down_v, part_v,
+    st_send, st_recv, left_send, right_send, left_recv, right_recv, left_out, right_out, so_send, centre_v, spread_v,
+    pairout_v, twice_v, up_v, down_v,
     load_sems, pair_sems, col_send, col_recv, fan_send, fan_recv,
     plane_sent, plane_came, kv_sent, kv_came, kv_relayed, q_sent, q_came, o_sent, o_came,
 ):
@@ -585,8 +585,7 @@
             ]
         return 0
 
-    bias_steps = depth // chunk
-    lax.fori_loop(0, bias_steps // 2, bias_step, 0)
+    lax.fori_loop(0, depth // chunk, bias_step, 0)
     for step in range(1, planes):
         plane_copies[step - 1].wait_recv()
         send_keys(step)
@@ -596,21 +595,27 @@
     def _():
         kv_recv[me_col, kind_mine] = kv_send[owner // 2, half_mine, kind_mine]
 
-    lax.fori_loop(bias_steps // 2, bias_steps, bias_step, 0)
     relays = [relay_query(peer) for peer in peers]
     for copy in relays:
         copy.wait_recv()
         copy.start()
-    for turn in range(parts):
+
+    def turn_part(turn, index):
+        return lax.rem(me_col // each + turn, parts) * each + index
+
+    def relay_turn(turn):
         for index in range(each):
-            part = lax.rem(me_col // each + turn, parts) * each + index
+            part = turn_part(turn, index)
             copy = relay_keys(part, kind_mine, part)
             own = jnp.logical_and(own_key, part == me_col)
             pl.when(jnp.logical_not(own))(copy.wait_recv)
             copy.start()
-            relays.append(copy)
+
+    relay_turn(0)
     gate_copies = to_cols(1, lambda to: gate_send.at[:, own_rows(to)], gate_recv.at[me_col])
     gate_recv[me_col] = gate_send[:, own_rows(me_col)]
+    relay_turn(1)
+    relays += [relay_keys(part, kind_mine, part) for part in range(col_size)]
 
     lane_row = lane_iota((2 * halves * heads, width))
     place = lax.broadcasted_iota(jnp.int32, (2 * halves * heads, width), 0)
@@ -707,6 +712,7 @@
             )
         for shift in range(1, col_size):
             o_copy(step, shift).start()
+        pl.when(turn + 2 < parts)(functools.partial(relay_turn, turn + 2))
         return 0
 
     lax.fori_loop(0, parts, attend_step, 0)
@@ -759,12 +765,12 @@
     low = lane_iota(first.shape) < shift
     left = jnp.where(low, first, pltpu.roll(second, shift, axis=1))
     right = jnp.where(low, pltpu.roll(first, shift, axis=1), second)
-    left_send[...] = left
-    right_send[...] = right
+    left_send[...] = left.astype(jnp.bfloat16)
+    right_send[...] = right.astype(jnp.bfloat16)
     right_copies = fan_copies(1, lambda half: right_send, right_recv)
     on_fan(right_copies, lambda copy: copy.start())
     left_copies = to_cols(4, lambda to: left_send, left_recv.at[me_col])
-    left_recv[me_col] = left
+    left_recv[me_col] = left.astype(jnp.bfloat16)
 
     @pl.when(mine)
     def _():
@@ -774,29 +780,22 @@
     for copy in left_copies:
         copy.wait_recv()
     so_copies = to_cols(5, lambda to: so_send, single_out.at[:, me_col])
-    own_copy = pltpu.make_async_copy(so_send, single_out.at[:, me_col], load_sems.at[0])
-    own_copy.start()
-    left = left_recv[...].reshape(depth, LANES)
+    single_out[:, me_col] = so_send[...]
+    left = left_recv[...].astype(jnp.float32).reshape(depth, LANES)
     turned = pltpu.roll(left, shift, axis=1)
     low = lane_iota(left.shape) < shift
     left_out[:depth] = jnp.where(low, left, turned)
     left_out[depth:] = jnp.where(low, turned, left)
-    right = right_recv[...].reshape(tile_cols, LANES)
+    right = right_recv[...].astype(jnp.float32).reshape(tile_cols, LANES)
     turned = pltpu.roll(right, shift, axis=1)
     right_out[...] = jnp.where(lane_iota(right.shape) // shift == half_mine, right, turned)
 
     twice_v[...] = twice(pairout_v[...])
     block = update_block
-    starts = part_v.shape[0] // (2 * block)
-
-    def part_copy(step):
-        rows = pl.ds(step * 2 * block, 2 * block)
-        return pltpu.make_async_copy(part_v.at[rows], part_out.at[rows], pair_sems.at[step])
-
     def update_step(step, _):
         first = step * 2 * block
         half = first // depth
-        part_v[pl.ds(first, 2 * block)] = update_rows(
+        pair_out[pl.ds(first, 2 * block)] = update_rows(
             lambda index: pair_v[half, pl.ds(first - half * depth + index * block, block)],
             lambda index: left_out[pl.ds(pl.multiple_of(first + index * block, 8), block)],
             right_out[...],
@@ -806,10 +805,9 @@
             up_v[...],
             down_v[...],
         )
-        part_copy(step).start()
         return 0
 
-    lax.fori_loop(0, starts, update_step, 0)
+    lax.fori_loop(0, tile_rows // (2 * block), update_step, 0)
 
     for copies in (q_copies, relays, plane_copies, gate_copies, st_copies, o_copies, left_copies, so_copies):
         for copy in copies:
@@ -818,95 +816,33 @@
     on_fan(right_copies, lambda copy: copy.wait_send())
     for copy in so_copies:
         copy.wait_recv()
-    own_copy.wait()
-    for step in range(starts):
-        part_copy(step).wait()
-
-
-def finish_kernel(
-    single, pair, part, left, right, w_pairout, w_up, w_down,
-    single_out, pair_out,
-    single_v, pair_v, part_v, done_v, left_v, right_v, pairout_v, up_v, down_v,
-    centre_v, twice_v, sems, out_sems,
-):
-    tile_rows, tile_cols, wide = pair.shape
-    done = part.shape[0]
-    block = (tile_rows - done) // 2
-    rows = pl.ds(done, 2 * block)
-    loads = [
-        pltpu.make_async_copy(source, target, sems.at[index])
-        for index, (source, target) in enumerate(
-            [
-                (w_pairout, pairout_v),
-                (pair.at[rows], pair_v),
-                (left.at[rows], left_v),
-                (right, right_v),
-                (w_up, up_v),
-                (w_down, down_v),
-                (part, part_v),
-                (single, single_v),
-            ]
-        )
-    ]
-    for copy in loads:
+
+
+def finish_kernel(single, pair, single_out, pair_out, sems):
+    copies = [pltpu.make_async_copy(single, single_out, sems.at[0])]
+    steps = sems.shape[0] - 1
+    rows = pair.shape[0] // steps
+    for step in range(steps):
+        part = pl.ds(step * rows, rows)
+        copies.append(
+            pltpu.make_async_copy(pair.at[part], pair_out.at[part], sems.at[1 + step])
+        )
+    for copy in copies:
         copy.start()
-    stores = [
-        pltpu.make_async_copy(part_v, pair_out.at[pl.ds(0, done)], out_sems.at[0]),
-        pltpu.make_async_copy(single_v, single_out, out_sems.at[1]),
-        pltpu.make_async_copy(done_v, pair_out.at[rows], out_sems.at[2]),
-    ]
-    centre_v[...] = centre_matrix(wide, 2)
-    for copy in loads[:6]:
+    for copy in copies:
         copy.wait()
-    twice_v[...] = twice(pairout_v[...])
-    for copy, store in zip(loads[6:], stores):
-        copy.wait()
-        store.start()
-    done_v[...] = update_rows(
-        lambda index: pair_v[index * block : (index + 1) * block],
-        lambda index: left_v[index * block : (index + 1) * block],
-        right_v[...],
-        block,
-        centre_v[...],
-        twice_v[...],
-        up_v[...],
-        down_v[...],
-    )
-    stores[2].start()
-    for store in stores:
-        store.wait()
-
-
-def finish(single, pair, part, left, right, w_pairout, w_up, w_down):
-    tile_rows, tile_cols, wide = pair.shape
-    done = part.shape[0]
-    any_spec = pl.BlockSpec(memory_space=pl.ANY)
-    bf16, f32 = jnp.bfloat16, jnp.float32
+
+
+def finish(single, pair):
     return pl.pallas_call(
         finish_kernel,
-        out_shape=(
-            jax.ShapeDtypeStruct(single.shape, bf16),
-            jax.ShapeDtypeStruct(pair.shape, bf16),
-        ),
-        in_specs=[any_spec] * 8,
-        out_specs=[any_spec] * 2,
-        scratch_shapes=[
-            pltpu.VMEM(single.shape, bf16),
-            pltpu.VMEM((tile_rows - done, tile_cols, wide), bf16),
-            pltpu.VMEM(part.shape, bf16),
-            pltpu.VMEM((tile_rows - done, tile_cols, wide), bf16),
-            pltpu.VMEM((tile_rows - done, wide), f32),
-            pltpu.VMEM(right.shape, f32),
-            pltpu.VMEM(w_pairout.shape, bf16),
-            pltpu.VMEM(w_up.shape, bf16),
-            pltpu.VMEM(w_down.shape, bf16),
-            pltpu.VMEM((2 * wide, 2 * wide), bf16),
-            pltpu.VMEM((2 * wide, 2 * wide), bf16),
-            pltpu.SemaphoreType.DMA((8,)),
-            pltpu.SemaphoreType.DMA((3,)),
-        ],
+        out_shape=tuple(jax.ShapeDtypeStruct(array.shape, array.dtype) for array in (single, pair)),
+        in_specs=[pl.BlockSpec(memory_space=pltpu.VMEM)] * 2,
+        out_specs=[pl.BlockSpec(memory_space=pl.ANY)] * 2,
+        scratch_shapes=[pltpu.SemaphoreType.DMA((9,))],
+        compiler_params=pltpu.CompilerParams(vmem_limit_bytes=8 * 1024 * 1024),
         name="finish",
-    )(single, pair, part, left, right, w_pairout, w_up, w_down)
+    )(single, pair)
 
 
 def attend(
@@ -920,21 +856,18 @@
     group = w_project.shape[2]
     steps = depth // 16
     parts = col_size // 2
-    part_rows = tile_rows - 2 * update_block
     stride = depth + 8
-    any_spec = pl.BlockSpec(memory_space=pl.ANY)
+    any_spec = pl.BlockSpec(memory_space=pltpu.HBM)
     vmem_spec = pl.BlockSpec(memory_space=pltpu.VMEM)
     bf16, f32 = jnp.bfloat16, jnp.float32
-    single_out, left, right, part = pl.pallas_call(
+    single_out, pair_out = pl.pallas_call(
         functools.partial(attend_kernel, row_size, col_size, heads, tile_cols, stride),
         out_shape=(
-            jax.ShapeDtypeStruct((halves, col_size, rows_each, width), bf16),
-            jax.ShapeDtypeStruct((tile_rows, wide), f32),
-            jax.ShapeDtypeStruct((tile_cols, wide), f32),
-            jax.ShapeDtypeStruct((part_rows, tile_cols, wide), bf16),
+            pltpu.VMEM((halves, col_size, rows_each, width), bf16),
+            pltpu.VMEM((tile_rows, tile_cols, wide), bf16),
         ),
         in_specs=[any_spec] * 10,
-        out_specs=[any_spec, vmem_spec, vmem_spec, any_spec],
+        out_specs=[vmem_spec] * 2,
         scratch_shapes=[
             pltpu.VMEM((tile_rows, width), bf16),
             pltpu.VMEM((halves, depth, tile_cols, wide), bf16),
@@ -954,10 +887,12 @@
             pltpu.VMEM((parts, col_size, halves * rows_each, width // parts), bf16),
             pltpu.VMEM((depth, LANES), f32),
             pltpu.VMEM((col_size, rows_each, LANES), f32),
-            pltpu.VMEM((rows_each, LANES), f32),
-            pltpu.VMEM((rows_each, LANES), f32),
-            pltpu.VMEM((col_size, rows_each, LANES), f32),
-            pltpu.VMEM((col_size, rows_each, LANES), f32),
+            pltpu.VMEM((rows_each, LANES), bf16),
+            pltpu.VMEM((rows_each, LANES), bf16),
+            pltpu.VMEM((col_size, rows_each, LANES), bf16),
+            pltpu.VMEM((col_size, rows_each, LANES), bf16),
+            pltpu.VMEM((tile_rows, wide), f32),
+            pltpu.VMEM((tile_cols, wide), f32),
             pltpu.VMEM((halves, rows_each, width), bf16),
             pltpu.VMEM((halves * wide, halves * wide), bf16),
             pltpu.VMEM((halves, 2 * LANES, width), bf16),
@@ -965,7 +900,6 @@
             pltpu.VMEM((2 * wide, 2 * wide), bf16),
             pltpu.VMEM(w_up.shape, bf16),
             pltpu.VMEM(w_down.shape, bf16),
-            pltpu.VMEM((part_rows, tile_cols, wide), bf16),
             pltpu.SemaphoreType.DMA((12 + halves,)),
             pltpu.SemaphoreType.DMA((steps,)),
             pltpu.SemaphoreType.DMA((6, col_size - 1)),
@@ -982,21 +916,29 @@
             pltpu.SemaphoreType.DMA((parts, col_size - 1)),
             pltpu.SemaphoreType.DMA((parts, col_size - 1)),
         ],
-        compiler_params=pltpu.CompilerParams(collective_id=3, has_side_effects=True),
+        compiler_params=pltpu.CompilerParams(
+            collective_id=3, has_side_effects=True, vmem_limit_bytes=40 * 1024 * 1024
+        ),
         name="attend",
     )(
-        single,
-        pair,
-        mask.reshape(mask.shape[0] // LANES, LANES),
-        w_bias.T,
-        w_project,
-        w_out,
-        w_factors,
-        w_pairout,
-        w_up,
-        w_down,
-    )
-    return single_out.reshape(tile_rows, width), left, right, part
+        *(
+            pltpu.with_memory_space_constraint(array, pltpu.HBM)
+            for array in (
+                single,
+                pair,
+                mask.reshape(mask.shape[0] // LANES, LANES),
+                w_bias.T,
+                w_project,
+                w_out,
+                w_factors,
+                w_pairout,
+                w_up,
+                w_down,
+            )
+        )
+    )
+    single_out, pair_out = finish(single_out, pair_out)
+    return single_out.reshape(tile_rows, width), pair_out
 
 
 def fits(row_size, col_size, single, pair, mask, w_bias, w_project, w_factors):
@@ -1023,11 +965,10 @@
     single, pair, residue_mask, w_bias, w_project, w_out, w_factors, w_pairout, w_up, w_down
 ):
     shape = pair.shape
-    single_out, left, right, part = attend(
+    return attend(
         single, pair.reshape(2, shape[0] // 2, *shape[1:]), residue_mask,
         w_bias, w_project, w_out, w_factors, w_pairout, w_up, w_down, row_size, col_size,
     )
-    return tuple(finish(single_out, pair, part, left, right, w_pairout, w_up, w_down))
 
 
 def dispatch(row_size, col_size, *arrays):

time: 44.5 us -> 40.5 us (0.910)
  Pallas kernels: 43.7 us -> 39.7 us
    pallas_call x1, Pallas kernels: 4.25 us -> 1.47 us  [finish(): pl.pallas_call(finish_kernel, out_shape=tuple((jax.ShapeDtypeStruct(array...]
    pallas_call x1, Pallas kernels: 39.4 us -> 38.3 us  [attend(): pl.pallas_call(functools.partial(attend_kernel, row_size, col_size, heads...]
where the time goes in v6:
time: 40.5 us; the launch traced here: 40.4 us
  Pallas kernels  39.7 us (98%)
  between operations  0.64 us (2%)
    pallas_call x1, Pallas kernels, attend(): pl.pallas_call(functools.partial(attend_kernel, row_size, col_size, heads...  38.3 us
    pallas_call x1, Pallas kernels, finish(): pl.pallas_call(finish_kernel, out_shape=tuple((jax.ShapeDtypeStruct(array...  1.47 us

profile of v6, /device:TPU:0, one launch (start us, length us, event | category | flops | bytes accessed | tf_op | source)
XLA Modules:
  0.0 40.4 jit_solution(17883221883044959925)
XLA Ops:
  0.6 38.3 %attend.1 = (bf16[2,8,8,1024]{3,2,1,0:T(8,128)(2,1)S(1)}, bf16[128,64,128]{2,1,0:T(8,128)(2,1)S(1)}) custom-call(bf16[128,1024]{1,0:T(8,128)(2,1)} %single.1, bf16[2,64,64,128]{3,2,1,0:T(8,128)(2,1)} %bitcast.4, s32[4,128]{1,0:T(4,128)} %bitcast.6, bf16[32,128]{1,0:T(8,128)(2,1)} %bitcast.5, bf16[4,1024,128]{2,1,0:T(8,128)(2,1)} %w_project.1, ...), custom_call_target="tpu_custom_call" | custom-call | tf_op jit(solution)/shard_map/attend/pallas_call | solution.py:863
  38.9 1.5 %finish.1 = (bf16[2,8,8,1024]{3,2,1,0:T(8,128)(2,1)}, bf16[128,64,128]{2,1,0:T(8,128)(2,1)}) custom-call(bf16[2,8,8,1024]{3,2,1,0:T(8,128)(2,1)S(1)} %get-tuple-element.6.single, bf16[128,64,128]{2,1,0:T(8,128)(2,1)S(1)} %get-tuple-element.7.pair), custom_call_target="tpu_custom_call" | custom-call | tf_op jit(solution)/shard_map/finish/pallas_call | solution.py:837

commit v7 on v6

--- a/solution.py
+++ b/solution.py
@@ -312,6 +312,14 @@
         square = jnp.sum(part * part, axis=1, keepdims=True) * (1.0 / wide)
         parts.append((part * lax.rsqrt(square + epsilon)).astype(jnp.bfloat16))
     return parts
+
+
+def exchange(index, turn, size):
+    total, bit = 0, 1
+    while bit < size:
+        total = total + lax.rem(index // bit + turn // bit, 2) * bit
+        bit *= 2
+    return total
 
 
 def twice(weights):
@@ -502,7 +510,14 @@
     loads[1].wait()
     q_recv[me_col] = project(0).astype(jnp.bfloat16)
     pl.semaphore_wait(barrier, total - 1)
-    peers = [lax.rem(me_col + 2 * step, col_size) for step in range(1, col_size // 2)]
+    parts, _, _, part_width = o_send.shape
+    each = part_width // group
+    col_side = lax.rem(me_col, each)
+
+    def turn_step(turn):
+        return exchange(me_col // each, turn, parts)
+
+    peers = [turn_step(turn) * each + col_side for turn in range(1, parts)]
     q_copies = [send_query(me_col, to, slot) for slot, to in enumerate(peers)]
     q_copies.append(send_query(me_col, col_mate, len(peers)))
     for copy in q_copies:
@@ -559,10 +574,6 @@
     loads[5].wait()
     loads[6].wait()
 
-    parts, _, _, part_width = o_send.shape
-    each = part_width // group
-    col_side = lax.rem(me_col, each)
-
     def relay_query(part):
         return send_query(part, col_mate, col_size // 2 + part // each)
 
@@ -595,27 +606,39 @@
     def _():
         kv_recv[me_col, kind_mine] = kv_send[owner // 2, half_mine, kind_mine]
 
+    def relay_keys_turn(turn):
+        for index in range(each):
+            part = turn_step(turn) * each + index
+            copy = relay_keys(part, kind_mine, part)
+            own = jnp.logical_and(own_key, part == me_col)
+            pl.when(jnp.logical_not(own))(copy.wait_recv)
+            copy.start()
+
+    same_plane = owner // 2 == me_plane
+    pl.when(same_plane)(functools.partial(relay_keys_turn, 0))
     relays = [relay_query(peer) for peer in peers]
     for copy in relays:
         copy.wait_recv()
         copy.start()
-
-    def turn_part(turn, index):
-        return lax.rem(me_col // each + turn, parts) * each + index
-
-    def relay_turn(turn):
-        for index in range(each):
-            part = turn_part(turn, index)
-            copy = relay_keys(part, kind_mine, part)
-            own = jnp.logical_and(own_key, part == me_col)
-            pl.when(jnp.logical_not(own))(copy.wait_recv)
-            copy.start()
-
-    relay_turn(0)
-    gate_copies = to_cols(1, lambda to: gate_send.at[:, own_rows(to)], gate_recv.at[me_col])
+    pl.when(jnp.logical_not(same_plane))(functools.partial(relay_keys_turn, 0))
+    relay_keys_turn(1)
+    relays += [relay_keys(part, kind_mine, part) for part in range(col_size)]
+
+    def gate_copy(shift):
+        to = lax.rem(me_col + shift, col_size)
+        return pltpu.make_async_remote_copy(
+            src_ref=gate_send.at[:, own_rows(to)],
+            dst_ref=gate_recv.at[me_col],
+            send_sem=col_send.at[1, shift - 1],
+            recv_sem=col_recv.at[1, shift - 1],
+            device_id={"cols": to},
+            device_id_type=pl.DeviceIdType.MESH,
+        )
+
+    gate_copies = [gate_copy(shift) for shift in range(1, col_size)]
+    for copy in gate_copies:
+        copy.start()
     gate_recv[me_col] = gate_send[:, own_rows(me_col)]
-    relay_turn(1)
-    relays += [relay_keys(part, kind_mine, part) for part in range(col_size)]
 
     lane_row = lane_iota((2 * halves * heads, width))
     place = lax.broadcasted_iota(jnp.int32, (2 * halves * heads, width), 0)
@@ -699,8 +722,19 @@
             device_id_type=pl.DeviceIdType.MESH,
         )
 
+    def st_copy(shift):
+        to = lax.rem(me_col + shift, col_size)
+        return pltpu.make_async_remote_copy(
+            src_ref=st_send.at[own_rows(to)],
+            dst_ref=st_recv.at[me_col],
+            send_sem=col_send.at[2, shift - 1],
+            recv_sem=col_recv.at[2, shift - 1],
+            device_id={"cols": to},
+            device_id_type=pl.DeviceIdType.MESH,
+        )
+
     def attend_step(turn, _):
-        step = lax.rem(me_col // each + turn, parts)
+        step = turn_step(turn)
         far = step * each + 1 - col_side
         relay_query(far).wait_recv()
         for index in range(each):
@@ -710,13 +744,19 @@
             o_send[step, :, :, index * group : (index + 1) * group] = attend_part(
                 step * each + index
             )
+
+        @pl.when(turn == parts - 1)
+        def _():
+            for shift in range(1, col_size):
+                st_copy(shift).start()
+
         for shift in range(1, col_size):
             o_copy(step, shift).start()
-        pl.when(turn + 2 < parts)(functools.partial(relay_turn, turn + 2))
+        pl.when(turn + 2 < parts)(functools.partial(relay_keys_turn, turn + 2))
         return 0
 
     lax.fori_loop(0, parts, attend_step, 0)
-    st_copies = to_cols(2, lambda to: st_send.at[own_rows(to)], st_recv.at[me_col])
+    st_copies = [st_copy(shift) for shift in range(1, col_size)]
     st_recv[me_col] = st_send[own_rows(me_col)]
     for step in range(parts):
         o_recv[step, me_col] = o_send[step, me_col]
@@ -955,6 +995,7 @@
         and tile_cols % (8 * col_size) == 0
         and col_size == 2 * row_size
         and row_size % 2 == 0
+        and col_size & (col_size - 1) == 0
         and tile_cols % (2 * update_block) == 0
         and mask.shape[0] % LANES == 0
     )

time: 40.5 us -> 39.9 us (0.985)
  Pallas kernels: 39.7 us -> 39.1 us
    pallas_call x1, Pallas kernels: 38.3 us -> 37.7 us  [attend(): pl.pallas_call(functools.partial(attend_kernel, row_size, col_size, heads...]
where the time goes in v7:
time: 39.9 us; the launch traced here: 39.8 us
  Pallas kernels  39.1 us (98%)
  between operations  0.64 us (2%)
    pallas_call x1, Pallas kernels, attend(): pl.pallas_call(functools.partial(attend_kernel, row_size, col_size, heads...  37.7 us
    pallas_call x1, Pallas kernels, finish(): pl.pallas_call(finish_kernel, out_shape=tuple((jax.ShapeDtypeStruct(array...  1.47 us

profile of v7, /device:TPU:0, one launch (start us, length us, event | category | flops | bytes accessed | tf_op | source)
XLA Modules:
  0.0 39.8 jit_solution(15649708225859439452)
XLA Ops:
  0.6 37.7 %attend.1 = (bf16[2,8,8,1024]{3,2,1,0:T(8,128)(2,1)S(1)}, bf16[128,64,128]{2,1,0:T(8,128)(2,1)S(1)}) custom-call(bf16[128,1024]{1,0:T(8,128)(2,1)} %single.1, bf16[2,64,64,128]{3,2,1,0:T(8,128)(2,1)} %bitcast.4, s32[4,128]{1,0:T(4,128)} %bitcast.6, bf16[32,128]{1,0:T(8,128)(2,1)} %bitcast.5, bf16[4,1024,128]{2,1,0:T(8,128)(2,1)} %w_project.1, ...), custom_call_target="tpu_custom_call" | custom-call | tf_op jit(solution)/shard_map/attend/pallas_call | solution.py:903
  38.3 1.5 %finish.1 = (bf16[2,8,8,1024]{3,2,1,0:T(8,128)(2,1)}, bf16[128,64,128]{2,1,0:T(8,128)(2,1)}) custom-call(bf16[2,8,8,1024]{3,2,1,0:T(8,128)(2,1)S(1)} %get-tuple-element.6.single, bf16[128,64,128]{2,1,0:T(8,128)(2,1)S(1)} %get-tuple-element.7.pair), custom_call_target="tpu_custom_call" | custom-call | tf_op jit(solution)/shard_map/finish/pallas_call | solution.py:877

commit v8 on v7

--- a/solution.py
+++ b/solution.py
@@ -288,7 +288,7 @@
 
 LANES = 128
 excluded = -1e30
-update_block = 16
+update_block = 32
 
 
 def lane_iota(shape):
@@ -359,7 +359,7 @@
     single_out, pair_out,
     single_v, pair_v, mask_v, bias_w, project_v, out_v, factors_v, own_single,
     kv_send, kv_recv, q_recv, gate_send, gate_recv, bias_v, o_send, o_recv,
-    st_send, st_recv, left_send, right_send, left_recv, right_recv, left_out, right_out, so_send, centre_v, spread_v,
+    st_send, st_recv, left_send, right_send, left_recv, right_recv, left_out, right_out, so_send, bias_t, st_rows, centre_v, spread_v,
     pairout_v, twice_v, up_v, down_v,
     load_sems, pair_sems, col_send, col_recv, fan_send, fan_recv,
     plane_sent, plane_came, kv_sent, kv_came, kv_relayed, q_sent, q_came, o_sent, o_came,
@@ -566,7 +566,7 @@
 
     send_keys(0)
     loads[4].wait()
-    gate_send[...] = jax.nn.sigmoid(project(3)).reshape(halves, depth, group)
+    gate_send[...] = jax.nn.sigmoid(project(3)).astype(jnp.bfloat16).reshape(gate_send.shape)
 
     def own_rows(to):
         return pl.ds(pl.multiple_of(to * rows_each, rows_each), rows_each)
@@ -597,6 +597,13 @@
         return 0
 
     lax.fori_loop(0, depth // chunk, bias_step, 0)
+    lane_row = lane_iota((2 * halves * heads, width))
+    place = lax.broadcasted_iota(jnp.int32, (2 * halves * heads, width), 0)
+    for half in range(halves):
+        picked = jnp.where(place == half * heads + lane_row // head_width, 1.0, 0.0)
+        spread_v[half, :LANES] = picked.astype(jnp.bfloat16)
+        spread_v[half, LANES:] = picked.astype(jnp.bfloat16)
+
     for step in range(1, planes):
         plane_copies[step - 1].wait_recv()
         send_keys(step)
@@ -614,6 +621,16 @@
             pl.when(jnp.logical_not(own))(copy.wait_recv)
             copy.start()
 
+    st_rows[...] = jnp.zeros_like(st_rows)
+
+    def turn_bias(turn, _):
+        for index in range(each * heads_here):
+            head = turn_step(turn) * each * heads_here + index
+            rows = bias_v[pl.ds(pl.multiple_of(head * stride, 8), depth), :].T
+            bias_t[head] = jnp.concatenate([rows[:tile_cols], rows[tile_cols:]], axis=1)
+        return 0
+
+    lax.fori_loop(0, parts, turn_bias, 0)
     same_plane = owner // 2 == me_plane
     pl.when(same_plane)(functools.partial(relay_keys_turn, 0))
     relays = [relay_query(peer) for peer in peers]
@@ -627,7 +644,7 @@
     def gate_copy(shift):
         to = lax.rem(me_col + shift, col_size)
         return pltpu.make_async_remote_copy(
-            src_ref=gate_send.at[:, own_rows(to)],
+            src_ref=gate_send.at[:, to],
             dst_ref=gate_recv.at[me_col],
             send_sem=col_send.at[1, shift - 1],
             recv_sem=col_recv.at[1, shift - 1],
@@ -638,75 +655,43 @@
     gate_copies = [gate_copy(shift) for shift in range(1, col_size)]
     for copy in gate_copies:
         copy.start()
-    gate_recv[me_col] = gate_send[:, own_rows(me_col)]
-
-    lane_row = lane_iota((2 * halves * heads, width))
-    place = lax.broadcasted_iota(jnp.int32, (2 * halves * heads, width), 0)
-    for half in range(halves):
-        picked = jnp.where(place == half * heads + lane_row // head_width, 1.0, 0.0)
-        spread_v[half, :LANES] = picked.astype(jnp.bfloat16)
-        spread_v[half, LANES:] = picked.astype(jnp.bfloat16)
+    gate_recv[me_col] = gate_send[:, me_col]
 
     length = jnp.sum(jnp.sum(mask_v[...], axis=1, keepdims=True), axis=0, keepdims=True)
-    lane = lane_iota((depth, LANES))
-    low = lane < tile_cols
-    valid = me_col * tile_cols + lax.rem(lane, tile_cols) < length
+    key_place = lax.broadcasted_iota(jnp.int32, (tile_cols, tile_rows), 0)
+    valid = me_col * tile_cols + key_place < length
     head_of = lane_iota((tile_cols, group)) // head_width
     head_masks = [
         jnp.where(head_of == head, 1.0, 0.0).astype(jnp.bfloat16) for head in range(heads_here)
     ]
-    zeros = jnp.zeros((tile_cols, group), jnp.bfloat16)
     scale = 1.0 / math.sqrt(head_width)
-    st_send[...] = jnp.zeros_like(st_send)
-    block_place = lax.broadcasted_iota(jnp.int32, (heads_here * LANES, LANES), 0) // tile_cols
-    block_target = (
-        halves * heads + lax.rem(block_place, halves) * heads + block_place // halves
-    )
-    block_lane = lane_iota((heads_here * LANES, LANES))
 
     def attend_part(part):
-        query = q_recv[part]
-        query = jnp.concatenate([query[:depth], query[depth:]], axis=1)
         key, value = kv_recv[part, 0], kv_recv[part, 1]
-        weights, value_rows = [], []
-        stats = st_send[...]
-        for first in range(0, heads_here, 2):
-            key_rows = []
-            for head in (first, first + 1):
-                masked = key * head_masks[head]
-                key_rows.append(jnp.concatenate([masked, zeros], axis=1))
-                key_rows.append(jnp.concatenate([zeros, masked], axis=1))
-            raw = lax.dot_general(
-                query,
-                jnp.concatenate(key_rows, axis=0),
-                (((1,), (1,)), ((), ())),
-                preferred_element_type=jnp.float32,
-            )
-            for head in (first, first + 1):
-                index = part * heads_here + head
-                bias = bias_v[pl.ds(pl.multiple_of(index * stride, 8), depth), :]
-                scores = raw[:, (head - first) * LANES : (head - first + 1) * LANES] * scale + bias
-                scores = jnp.where(valid, scores, excluded)
-                top0 = jnp.max(jnp.where(low, scores, excluded), axis=1, keepdims=True)
-                top1 = jnp.max(jnp.where(low, excluded, scores), axis=1, keepdims=True)
-                weights.append(
-                    jnp.exp(scores - jnp.where(low, top0, top1)).astype(jnp.bfloat16)
-                )
-                stats = jnp.where(lane == index, top0, stats)
-                stats = jnp.where(lane == heads + index, top1, stats)
+        raw = lax.dot_general(
+            jnp.concatenate([key * mask for mask in head_masks], axis=0),
+            q_recv[part],
+            (((1,), (1,)), ((), ())),
+            preferred_element_type=jnp.float32,
+        )
+        weights = []
         for head in range(heads_here):
-            masked = value * head_masks[head]
-            value_rows.append(jnp.concatenate([masked, zeros], axis=1))
-            value_rows.append(jnp.concatenate([zeros, masked], axis=1))
-        weights = jnp.concatenate(weights, axis=1)
-        mixed = jnp.dot(
-            weights, jnp.concatenate(value_rows, axis=0), preferred_element_type=jnp.float32
-        )
-        ones = jnp.where(block_lane == block_target + part * heads_here, 1.0, 0.0)
-        sums = jnp.dot(weights, ones.astype(jnp.bfloat16), preferred_element_type=jnp.float32)
-        st_send[...] = stats + sums
+            index = part * heads_here + head
+            scores = raw[head * tile_cols : (head + 1) * tile_cols] * scale + bias_t[index]
+            scores = jnp.where(valid, scores, excluded)
+            top = jnp.max(scores, axis=0, keepdims=True)
+            weight = jnp.exp(scores - top)
+            st_rows[pl.ds(index, 1), :] = top
+            st_rows[pl.ds(halves * heads + index, 1), :] = jnp.sum(weight, axis=0, keepdims=True)
+            weights.append(weight.astype(jnp.bfloat16))
+        mixed = lax.dot_general(
+            jnp.concatenate(weights, axis=0),
+            jnp.concatenate([value * mask for mask in head_masks], axis=0),
+            (((0,), (0,)), ((), ())),
+            preferred_element_type=jnp.float32,
+        )
         pieces = [
-            mixed[:, half * group : (half + 1) * group].reshape(col_size, rows_each, group)
+            mixed[half * depth : (half + 1) * depth].reshape(col_size, rows_each, group)
             for half in range(halves)
         ]
         return jnp.concatenate(pieces, axis=1).astype(jnp.bfloat16)
@@ -747,6 +732,8 @@
 
         @pl.when(turn == parts - 1)
         def _():
+            stats = st_rows[...].T
+            st_send[...] = stats[:depth] + pltpu.roll(stats[depth:], heads, axis=1)
             for shift in range(1, col_size):
                 st_copy(shift).start()
 
@@ -777,7 +764,11 @@
         jnp.dot(factor, spread_v[half], preferred_element_type=jnp.float32) for half in range(halves)
     ]
     gate = jnp.concatenate(
-        [gate_recv[part].reshape(halves * rows_each, group) for part in range(col_size)], axis=1
+        [
+            gate_recv[part].astype(jnp.float32).reshape(halves * rows_each, group)
+            for part in range(col_size)
+        ],
+        axis=1,
     )
     for copy in o_copies:
         copy.wait_recv()
@@ -920,8 +911,8 @@
             pltpu.VMEM((row_size // 2, halves, 2, tile_cols, group), bf16),
             pltpu.VMEM((col_size, 2, tile_cols, group), bf16),
             pltpu.VMEM((col_size, tile_rows, group), bf16),
-            pltpu.VMEM((halves, depth, group), f32),
-            pltpu.VMEM((col_size, halves, rows_each, group), f32),
+            pltpu.VMEM((halves, col_size, rows_each, group), bf16),
+            pltpu.VMEM((col_size, halves, rows_each, group), bf16),
             pltpu.VMEM((heads * stride, LANES), f32),
             pltpu.VMEM((parts, col_size, halves * rows_each, width // parts), bf16),
             pltpu.VMEM((parts, col_size, halves * rows_each, width // parts), bf16),
@@ -934,6 +925,8 @@
             pltpu.VMEM((tile_rows, wide), f32),
             pltpu.VMEM((tile_cols, wide), f32),
             pltpu.VMEM((halves, rows_each, width), bf16),
+            pltpu.VMEM((heads, tile_cols, tile_rows), f32),
+            pltpu.VMEM((4 * heads, tile_rows), f32),
             pltpu.VMEM((halves * wide, halves * wide), bf16),
             pltpu.VMEM((halves, 2 * LANES, width), bf16),
             pltpu.VMEM(w_pairout.shape, bf16),

time: 39.9 us -> 38.9 us (0.975)
  Pallas kernels: 39.1 us -> 38.1 us
    pallas_call x1, Pallas kernels: 37.7 us -> 36.7 us  [attend(): pl.pallas_call(functools.partial(attend_kernel, row_size, col_size, heads...]
where the time goes in v8:
time: 38.9 us; the launch traced here: 38.8 us
  Pallas kernels  38.1 us (98%)
  between operations  0.64 us (2%)
    pallas_call x1, Pallas kernels, attend(): pl.pallas_call(functools.partial(attend_kernel, row_size, col_size, heads...  36.7 us
    pallas_call x1, Pallas kernels, finish(): pl.pallas_call(finish_kernel, out_shape=tuple((jax.ShapeDtypeStruct(array...  1.47 us

profile of v8, /device:TPU:0, one launch (start us, length us, event | category | flops | bytes accessed | tf_op | source)
XLA Modules:
  0.0 38.8 jit_solution(2773789768444408807)
XLA Ops:
  0.6 36.7 %attend.1 = (bf16[2,8,8,1024]{3,2,1,0:T(8,128)(2,1)S(1)}, bf16[128,64,128]{2,1,0:T(8,128)(2,1)S(1)}) custom-call(bf16[128,1024]{1,0:T(8,128)(2,1)} %single.1, bf16[2,64,64,128]{3,2,1,0:T(8,128)(2,1)} %bitcast.4, s32[4,128]{1,0:T(4,128)} %bitcast.6, bf16[32,128]{1,0:T(8,128)(2,1)} %bitcast.5, bf16[4,1024,128]{2,1,0:T(8,128)(2,1)} %w_project.1, ...), custom_call_target="tpu_custom_call" | custom-call | tf_op jit(solution)/shard_map/attend/pallas_call | solution.py:894
  37.3 1.5 %finish.1 = (bf16[2,8,8,1024]{3,2,1,0:T(8,128)(2,1)}, bf16[128,64,128]{2,1,0:T(8,128)(2,1)}) custom-call(bf16[2,8,8,1024]{3,2,1,0:T(8,128)(2,1)S(1)} %get-tuple-element.6.single, bf16[128,64,128]{2,1,0:T(8,128)(2,1)S(1)} %get-tuple-element.7.pair), custom_call_target="tpu_custom_call" | custom-call | tf_op jit(solution)/shard_map/finish/pallas_call | solution.py:868

commit v9 on v8

--- a/solution.py
+++ b/solution.py
@@ -913,7 +913,7 @@
             pltpu.VMEM((col_size, tile_rows, group), bf16),
             pltpu.VMEM((halves, col_size, rows_each, group), bf16),
             pltpu.VMEM((col_size, halves, rows_each, group), bf16),
-            pltpu.VMEM((heads * stride, LANES), f32),
+            pltpu.VMEM(((heads + 1) * stride, LANES), f32),
             pltpu.VMEM((parts, col_size, halves * rows_each, width // parts), bf16),
             pltpu.VMEM((parts, col_size, halves * rows_each, width // parts), bf16),
             pltpu.VMEM((depth, LANES), f32),

time: 38.9 us -> 38.9 us (level)
  no operation moved by 1% of the time
where the time goes in v9:
time: 38.9 us; the launch traced here: 38.8 us
  Pallas kernels  38.1 us (98%)
  between operations  0.64 us (2%)
    pallas_call x1, Pallas kernels, attend(): pl.pallas_call(functools.partial(attend_kernel, row_size, col_size, heads...  36.7 us
    pallas_call x1, Pallas kernels, finish(): pl.pallas_call(finish_kernel, out_shape=tuple((jax.ShapeDtypeStruct(array...  1.47 us

profile of v9, /device:TPU:0, one launch (start us, length us, event | category | flops | bytes accessed | tf_op | source)
XLA Modules:
  0.0 38.8 jit_solution(14588003742735802481)
XLA Ops:
  0.6 36.7 %attend.1 = (bf16[2,8,8,1024]{3,2,1,0:T(8,128)(2,1)S(1)}, bf16[128,64,128]{2,1,0:T(8,128)(2,1)S(1)}) custom-call(bf16[128,1024]{1,0:T(8,128)(2,1)} %single.1, bf16[2,64,64,128]{3,2,1,0:T(8,128)(2,1)} %bitcast.4, s32[4,128]{1,0:T(4,128)} %bitcast.6, bf16[32,128]{1,0:T(8,128)(2,1)} %bitcast.5, bf16[4,1024,128]{2,1,0:T(8,128)(2,1)} %w_project.1, ...), custom_call_target="tpu_custom_call" | custom-call | tf_op jit(solution)/shard_map/attend/pallas_call | solution.py:894
  37.3 1.5 %finish.1 = (bf16[2,8,8,1024]{3,2,1,0:T(8,128)(2,1)}, bf16[128,64,128]{2,1,0:T(8,128)(2,1)}) custom-call(bf16[2,8,8,1024]{3,2,1,0:T(8,128)(2,1)S(1)} %get-tuple-element.6.single, bf16[128,64,128]{2,1,0:T(8,128)(2,1)S(1)} %get-tuple-element.7.pair), custom_call_target="tpu_custom_call" | custom-call | tf_op jit(solution)/shard_map/finish/pallas_call | solution.py:868
